TPU v7x, 512 devices: a whole 4x4x16 slice. The times are simulated.
512 devices in a mesh: mem: 4 (over z_lo), gx: 16 (over y, z_hi), gy: 8 (over x, core).
Axes of the slice: x: 4, y: 4, z: 16 (z_hi: 4, z_lo: 4; z = z_hi * 4 + z_lo), core: 2. Of those that a mesh axis runs over, the one named last changes fastest.
Arguments:
- initial_states: float32 [40, 4, 128, 1024], P('mem', None, 'gx', 'gy'), may hold values from -6 to 6
- diffusivity: float32 [4, 128, 1024], P(None, 'gx', 'gy'), may hold values from 0.04 to 0.24
- ocean_mask: int32 [128, 1024], P('gx', 'gy'), may hold values 0 or 1
- obs_values: float32 [4, 16, 32, 128], P(None, None, 'gx', 'gy'), may hold values from -6 to 6
- obs_variance: float32 [4, 16, 32, 128], P(None, None, 'gx', 'gy'), may hold values from 0.25 to 4
- obs_cells: int32 [4, 16, 32, 128], P(None, None, 'gx', 'gy'), may hold values from 0 to 31
- obs_blocks: int32 [5, 32, 128], P(None, 'gx', 'gy'), may hold values from 0 to 8, as said below
Outputs:
- analysis: float32 [40, 4, 128, 1024], P('mem', None, 'gx', 'gy')
Inputs may be any that keep to these rules, and one draw needn't show every extreme that they name: `ocean_mask`: 1 marks an ocean cell, 0 a land cell. `obs_cells`: the cell of the observation in its patch, row-major over 4 x 8 cells; several observations may share a cell. `obs_blocks`: for each patch, 5 different codes 3 * (r + 1) + (c + 1) of the patches at row offset r and column offset c, r and c in -1, 0, 1.
All inputs are finite; a program needn't handle non-finite values. No bound on the sum of `ocean_mask` on one device may be relied on, other than what follows from the above.
Results may differ from a plain program's by a relative error of at most 0.0003.
Values sent between devices are 32-bit elements; how exact they have to be, the bound alone decides.
A program may use at most 64 MiB of HBM per device.

v0:
```python
import jax
import jax.numpy as jnp
from jax import lax
from jax.experimental import pallas as pl
from jax.experimental.pallas import tpu as pltpu
from jax.sharding import PartitionSpec as P

MESH = pl.DeviceIdType.MESH
F32 = jnp.float32
NS_ITERS = 7
LEVELS = 4
OWN = 10
MEMBERS = 40
OBS = 16
AUX = 32
NEED = ((16, 64), (0, 80), (0, 64))


def gather_kernel(n_gx, n_gy, x_ref, aux_ref, g_ref, a_ref, ssem, rsem, asem, arsem, fsem, frsem, lsem):
    mem, gx, gy = lax.axis_index("mem"), lax.axis_index("gx"), lax.axis_index("gy")
    rows = (lax.rem(gx + n_gx - 1, n_gx), gx, lax.rem(gx + 1, n_gx))
    sides = (lax.rem(gy + n_gy - 1, n_gy), lax.rem(gy + 1, n_gy))
    there = [lax.rem(mem + o, LEVELS) for o in range(LEVELS)]
    back = [lax.rem(mem + LEVELS - o, LEVELS) for o in range(LEVELS)]

    barrier = pltpu.get_barrier_semaphore()
    count = 0
    for d in range(3):
        for o in range(LEVELS):
            if d == 1 and o == 0:
                continue
            pl.semaphore_signal(barrier, inc=1, device_id=(there[o], rows[d], gy), device_id_type=MESH)
            count += 1
    for side in sides:
        pl.semaphore_signal(barrier, inc=1, device_id=(mem, gx, side), device_id_type=MESH)
        count += 1

    own = pltpu.make_async_copy(x_ref.at[mem], g_ref.at[1, 1, mem], lsem.at[0])
    own_aux = pltpu.make_async_copy(aux_ref, a_ref.at[1, 1], lsem.at[1])
    own.start()
    own_aux.start()
    pl.semaphore_wait(barrier, count)

    sends = []

    def forward(source, dg, slot, part, index):
        for e, side in enumerate(sides):
            h = 2 if e == 0 else 0
            dst = a_ref.at[h, dg] if slot is None else g_ref.at[h, dg, slot, part]
            copy = pltpu.make_async_remote_copy(
                src_ref=source, dst_ref=dst, send_sem=fsem.at[e, dg, index], recv_sem=frsem.at[h // 2, dg, index],
                device_id=(mem, gx, side), device_id_type=MESH)
            copy.start()
            sends.append(copy)

    def scatter(d, o):
        part = pl.ds(*NEED[2 - d])
        copy = pltpu.make_async_remote_copy(
            src_ref=x_ref.at[there[o], part], dst_ref=g_ref.at[1, 2 - d, mem, part],
            send_sem=ssem.at[d, o], recv_sem=rsem.at[2 - d, o],
            device_id=(there[o], rows[d], gy), device_id_type=MESH)
        copy.start()
        sends.append(copy)

    for d in (0, 2):
        copy = pltpu.make_async_remote_copy(
            src_ref=aux_ref, dst_ref=a_ref.at[1, 2 - d], send_sem=asem.at[d], recv_sem=arsem.at[2 - d],
            device_id=(mem, rows[d], gy), device_id_type=MESH)
        copy.start()
        sends.append(copy)
    for o in range(LEVELS):
        scatter(0, o)
        scatter(2, o)
    for o in range(1, LEVELS):
        scatter(1, o)
    forward(aux_ref, 1, None, None, LEVELS)
    forward(x_ref.at[mem], 1, mem, pl.ds(0, 80), 0)

    def arrival(dg, o, source):
        part = pl.ds(*NEED[dg])
        return pltpu.make_async_remote_copy(
            src_ref=x_ref.at[0, part], dst_ref=g_ref.at[1, dg, source, part],
            send_sem=ssem.at[dg, o], recv_sem=rsem.at[dg, o],
            device_id=(mem, rows[dg], gy), device_id_type=MESH)

    for dg, o in [(1, 1), (1, 3), (1, 2)]:
        arrival(dg, o, back[o]).wait_recv()
        forward(g_ref.at[1, dg, back[o], pl.ds(*NEED[dg])], dg, back[o], pl.ds(*NEED[dg]), o)
    for dg in (0, 2):
        pltpu.make_async_remote_copy(
            src_ref=aux_ref, dst_ref=a_ref.at[1, dg], send_sem=asem.at[dg], recv_sem=arsem.at[dg],
            device_id=(mem, rows[dg], gy), device_id_type=MESH).wait_recv()
        forward(a_ref.at[1, dg], dg, None, None, LEVELS)
    for o in range(LEVELS):
        for dg in (0, 2):
            arrival(dg, o, back[o]).wait_recv()
            forward(g_ref.at[1, dg, back[o], pl.ds(*NEED[dg])], dg, back[o], pl.ds(*NEED[dg]), o)
    for h in (0, 2):
        for dg in range(3):
            for o in range(LEVELS):
                part = pl.ds(*NEED[dg])
                pltpu.make_async_remote_copy(
                    src_ref=x_ref.at[0, part], dst_ref=g_ref.at[h, dg, back[o], part],
                    send_sem=fsem.at[0, dg, o], recv_sem=frsem.at[h // 2, dg, o],
                    device_id=(mem, gx, sides[0]), device_id_type=MESH).wait_recv()
            pltpu.make_async_remote_copy(
                src_ref=aux_ref, dst_ref=a_ref.at[h, dg],
                send_sem=fsem.at[0, dg, LEVELS], recv_sem=frsem.at[h // 2, dg, LEVELS],
                device_id=(mem, gx, sides[0]), device_id_type=MESH).wait_recv()
    for copy in sends:
        copy.wait_send()
    own.wait()
    own_aux.wait()


def split(x):
    high = x.astype(jnp.bfloat16).astype(F32)
    return high, x - high


def mxu(a, b):
    return lax.dot_general(a, b, (((1,), (0,)), ((), ())), preferred_element_type=F32)


def mxu_nt(a, b):
    return lax.dot_general(a, b, (((1,), (1,)), ((), ())), preferred_element_type=F32)


def iota(shape, axis):
    return lax.broadcasted_iota(jnp.int32, shape, axis)


def block_of(lane):
    return jnp.where(lane < 40, 0, jnp.where(lane < 80, 1, jnp.where(lane < 120, 2, 3)))


def three_high(value, block):
    parts = [jnp.where(block == i, value, 0.0) for i in range(3)]
    return jnp.concatenate(parts + [jnp.zeros((8, value.shape[1]), F32)], axis=0)


def compute_kernel(n_gx, n_gy, g_ref, a_ref, ob_ref, out_ref, f0, f1, dif, wet, pt, mean, slab, wc, gram, tr, tv, ps, zs):
    gx, gy = lax.axis_index("gx"), lax.axis_index("gy")
    up = jnp.where(gx > 0, 1.0, 0.0).astype(F32)
    down = jnp.where(gx < n_gx - 1, 1.0, 0.0).astype(F32)
    west = jnp.where(gy > 0, 1.0, 0.0).astype(F32)
    east = jnp.where(gy < n_gy - 1, 1.0, 0.0).astype(F32)
    in_grid = (up, jnp.float32(1.0), down)
    lane1 = iota((1, 128), 1)
    beside = jnp.where(lane1 < 64, east, west)

    def both(h_of, dg):
        own = h_of(1) * in_grid[dg]
        side = jnp.where(lane1 < 64, h_of(2), h_of(0)) * (beside * in_grid[dg])
        return own, side

    for t in range(20):
        dg, r = (0, t + 2) if t < 6 else (1, t - 6) if t < 14 else (2, t - 14)
        main = 8 * r if r < 2 else 16 + 8 * r
        rest = 16 + 2 * r
        for s in range(LEVELS):
            own, side = both(lambda h: g_ref[h, dg, s, main:main + 8, :], dg)
            f0[t, 8 * s:8 * s + 8, 0:128] = own
            f0[t, 8 * s:8 * s + 8, 128:256] = side
            own, side = both(lambda h: g_ref[h, dg, s, rest:rest + 2, :], dg)
            f0[t, 32 + 2 * s:34 + 2 * s, 0:128] = own
            f0[t, 32 + 2 * s:34 + 2 * s, 128:256] = side
        own, side = both(lambda h: a_ref[h, dg, r:r + 1, :], dg)
        dif[t, :, 0:128] = own
        dif[t, :, 128:256] = side
        own, side = both(lambda h: a_ref[h, dg, 8 + r:9 + r, :], dg)
        wet[t, :, 0:128] = own
        wet[t, :, 128:256] = side

    def advance(src, t):
        c = src[t]
        around = src[t + 1] + src[t - 1]
        around = around + pltpu.roll(c, 255, 1) + pltpu.roll(c, 1, 1)
        return wet[t] * (c + dif[t] * (around - 4.0 * c))

    def first(t, carry):
        f1[t] = advance(f0, t)
        return carry

    lax.fori_loop(1, 19, first, 0)

    def second(p, carry):
        for r in range(4):
            value = advance(f1, 2 + 4 * p + r)
            m = jnp.sum(value, axis=0, keepdims=True) / MEMBERS
            q = value - m
            tail = jnp.where(iota((8, 256), 0) == 0, m, 0.0)
            for k in range(2):
                at = 512 * k + 128 * r
                pt[p, 0:40, at:at + 128] = q[:, 128 * k:128 * k + 128]
                pt[p, 40:48, at:at + 128] = tail[:, 128 * k:128 * k + 128]
            mean[p, :, 128 * r:128 * r + 128] = m[:, 0:128]
        return carry

    lax.fori_loop(0, 4, second, 0)

    lane2 = iota((1, 256), 1)
    inverse_of = []
    for p in range(4):
        dg, a = ((0, 1), (1, 0), (1, 1), (2, 0))[p]

        def rows_of(kind):
            at = 16 + (a * 3 + kind) * 2
            own = jnp.concatenate([a_ref[1, dg, at:at + 1, :], a_ref[1, dg, at + 1:at + 2, :]], axis=1)
            return own, jnp.where(lane1 < 64, a_ref[2, dg, at:at + 1, :], a_ref[0, dg, at + 1:at + 2, :])

        value, variance, cell = rows_of(0), rows_of(1), rows_of(2)
        found = []
        for k, (lane, shift) in enumerate(((lane2, 0), (lane1, jnp.where(lane1 < 64, 0, 64)))):
            c = cell[k].astype(jnp.int32)
            target = (c >> 3) * 128 + ((lane >> 4) << 3) + (c & 7) + shift
            hot = jnp.where(iota((512, lane.shape[1]), 0) == target, 1.0, 0.0).astype(F32)
            high, low = split(pt[p, :, 512 * k:512 * k + 512])
            both_parts = mxu(jnp.concatenate([high, low], axis=0), hot)
            found.append(both_parts[0:48] + both_parts[48:96])
        whole = jnp.concatenate(found, axis=1)
        values = jnp.concatenate(value, axis=1)
        tail = whole[40:48]
        tail = jnp.where(iota((8, 384), 0) == 0, values - tail, 0.0)
        slab[p, 0:40, :] = whole[0:40]
        slab[p, 40:48, :] = tail
        inside = jnp.concatenate([jnp.ones((1, 256), F32), beside], axis=1) * in_grid[dg]
        inverse_of.append(inside / jnp.concatenate(variance, axis=1))

    third = lax.rem(iota((1, 384), 1) >> 4, 3)
    for a in range(2):
        for r in range(3):
            near = []
            for c in range(3):
                code = 3 * r + c
                taper = 1.0 if code == 4 else 0.5 if (r == 1 or c == 1) else 0.25
                chosen = jnp.zeros((1, 256), F32)
                for s in range(5):
                    at = (s * 2 + a) * 2
                    blocks = jnp.concatenate([ob_ref[at:at + 1, :], ob_ref[at + 1:at + 2, :]], axis=1)
                    chosen = chosen + jnp.where(blocks == code, taper, 0.0)
                chosen = jnp.concatenate([chosen, jnp.zeros((1, 128), F32)], axis=1)
                near.append(pltpu.roll(chosen, (16 * (c - 1)) % 384, 1) if c != 1 else chosen)
            for i in range(3):
                which = lax.rem(third + 4 - i, 3)
                w = jnp.where(which == 0, near[0], jnp.where(which == 1, near[1], near[2]))
                wc[a, 3 * r + i:3 * r + i + 1, :] = w * inverse_of[a + r]

    slot = lane1 >> 4
    block = block_of(lane1)
    own_slot = [(slot >= i) & (slot <= i + 2) for i in range(3)]
    diagonal = (lane1 - 40 * block == iota((40, 128), 0)) & (lane1 < 120)
    for g in range(6):
        turn = (16 - 48 * g) % 384

        def window(x):
            return (pltpu.roll(x, turn, 1) if turn else x)[:, 0:128]

        parts = [window(slab[p]) for p in range(4)]
        for a in range(2):
            weights = window(wc[a])
            left = jnp.concatenate(parts[a:a + 3], axis=1)
            right = []
            for i in range(3):
                right.append(jnp.concatenate([
                    parts[a + r][0:40] * jnp.where(own_slot[i], weights[3 * r + i:3 * r + i + 1], 0.0)
                    for r in range(3)], axis=1))
            right.append(jnp.zeros((8, 384), F32))
            right = jnp.concatenate(right, axis=0)
            lh, ll = split(left)
            rh, rl = split(right)
            o = mxu_nt(jnp.concatenate([lh, ll], axis=0), jnp.concatenate([rh, rl], axis=0))
            o = o[0:48] + o[48:96]
            o = o[:, 0:128] + o[:, 128:256]
            system = jnp.where(diagonal, 1.0, 0.0) + o[0:40] / (MEMBERS - 1.0)
            n = a * 6 + g
            gram[n, 0:40, :] = system
            gram[n, 40:48, :] = o[40:48] / (MEMBERS - 1.0)
            tr[n:n + 1, :] = jnp.sum(jnp.where(diagonal, system, 0.0), axis=0, keepdims=True)

    rows = tr[...]
    sums = [jnp.sum(jnp.where(block == i, rows, 0.0), axis=1, keepdims=True) for i in range(3)]
    tv[...] = jnp.where(block == 0, sums[0], jnp.where(block == 1, sums[1], sums[2]))
    for n in range(12):
        ps[n] = gram[n, 0:40, :] / tv[n:n + 1, :]
        zs[n] = jnp.where(diagonal, 1.0, 0.0)

    wide = jnp.concatenate([block, block], axis=1)

    def sweep(step, carry):
        for n in range(12):
            p, z = ps[n], zs[n]
            pair = jnp.concatenate(split(p), axis=1)
            stacked = three_high(pair, wide)
            right = jnp.concatenate([stacked, stacked], axis=0)
            o = mxu(jnp.concatenate([pair, jnp.concatenate(split(z), axis=1)], axis=0), right)
            o = o[:, 0:128] + o[:, 128:256]
            zs[n] = 1.5 * z - 0.5 * o[40:80]
            q = 1.5 * p - 0.5 * o[0:40]
            o = mxu(jnp.concatenate(split(q), axis=1), right)
            ps[n] = 1.5 * q - 0.5 * (o[:, 0:128] + o[:, 128:256])
        return carry

    lax.fori_loop(0, NS_ITERS - 1, sweep, 0)

    ones = jnp.where((block_of(iota((128, 128), 0)) == block) & (lane1 < 120), 1.0, 0.0).astype(F32)
    ones = jnp.concatenate([ones, ones], axis=0)
    patch = lax.rem(iota((1, 512), 1), 128) >> 3
    for a in range(2):
        total = jnp.zeros((40, 512), F32)
        ph, plow = split(pt[a + 1, 0:40, 0:512])
        for g in range(6):
            n = a * 6 + g
            p, z = ps[n], zs[n]
            pair = jnp.concatenate(split(p), axis=1)
            stacked = three_high(pair, wide)
            o = mxu(jnp.concatenate(split(z), axis=1), jnp.concatenate([stacked, stacked], axis=0))
            z = 1.5 * z - 0.5 * (o[:, 0:128] + o[:, 128:256])
            spread = z / jnp.sqrt(tv[n:n + 1, :])
            partial = mxu(jnp.concatenate(split(spread * gram[n, 40:41, :]), axis=1), ones)
            centre = jnp.sum(spread * partial, axis=0, keepdims=True)
            th, tl = split(spread + centre)
            high = three_high_by(ph, patch, 3 * g)
            low = three_high_by(plow, patch, 3 * g)
            total = total + mxu(jnp.concatenate([th, tl, th], axis=1), jnp.concatenate([high, high, low], axis=0))
        total = total + mean[a + 1]
        for r in range(4):
            value = total[:, 128 * r:128 * r + 128]
            for s in range(LEVELS):
                out_ref[s, 0:8, 4 * a + r, :] = value[8 * s:8 * s + 8]
                out_ref[s, 8:10, 4 * a + r, :] = value[32 + 2 * s:34 + 2 * s]


def three_high_by(value, patch, first):
    parts = [jnp.where(patch == first + i, value, 0.0) for i in range(3)]
    return jnp.concatenate(parts + [jnp.zeros((8, value.shape[1]), F32)], axis=0)


def return_kernel(y_ref, out_ref, ssem, rsem, lsem):
    mem, gx, gy = lax.axis_index("mem"), lax.axis_index("gx"), lax.axis_index("gy")
    there = [lax.rem(mem + o, LEVELS) for o in range(LEVELS)]
    back = [lax.rem(mem + LEVELS - o, LEVELS) for o in range(LEVELS)]
    barrier = pltpu.get_barrier_semaphore()
    for o in range(1, LEVELS):
        pl.semaphore_signal(barrier, inc=1, device_id=(there[o], gx, gy), device_id_type=MESH)
    own = pltpu.make_async_copy(y_ref.at[mem], out_ref.at[mem], lsem.at[0])
    own.start()
    pl.semaphore_wait(barrier, LEVELS - 1)
    sends = []
    for o in range(1, LEVELS):
        copy = pltpu.make_async_remote_copy(
            src_ref=y_ref.at[there[o]], dst_ref=out_ref.at[mem], send_sem=ssem.at[o], recv_sem=rsem.at[o],
            device_id=(there[o], gx, gy), device_id_type=MESH)
        copy.start()
        sends.append(copy)
    for o in range(1, LEVELS):
        pltpu.make_async_remote_copy(
            src_ref=y_ref.at[0], dst_ref=out_ref.at[back[o]], send_sem=ssem.at[o], recv_sem=rsem.at[o],
            device_id=(there[o], gx, gy), device_id_type=MESH).wait_recv()
    for copy in sends:
        copy.wait_send()
    own.wait()


def prepare(initial_states, diffusivity, ocean_mask, obs_values, obs_variance, obs_cells, obs_blocks):
    x = initial_states.transpose(1, 2, 0, 3)
    main = x[:, :, :8]
    chunks = jnp.concatenate([
        main[:, :2].reshape(LEVELS, 16, 128), x[:, :, 8:].reshape(LEVELS, 16, 128),
        main[:, 2:].reshape(LEVELS, 48, 128)], axis=1)
    level = lax.axis_index("mem")

    def lanes(v):
        v = lax.dynamic_index_in_dim(v, level, 0, keepdims=False).astype(F32)
        return v.transpose(1, 2, 0).reshape(2, 2, 128)

    obs = jnp.stack([lanes(obs_values), lanes(obs_variance), lanes(obs_cells)], axis=1).reshape(12, 128)
    aux = jnp.concatenate([
        lax.dynamic_index_in_dim(diffusivity, level, 0, keepdims=False), ocean_mask.astype(F32), obs,
        jnp.zeros((4, 128), F32)], axis=0)
    blocks = jnp.broadcast_to(obs_blocks[:, :, :, None], obs_blocks.shape + (OBS,)).reshape(20, 128)
    return chunks, aux, blocks


def compute_call(n_gx, n_gy, gathered, aux, blocks, **kw):
    vmem = pl.BlockSpec(memory_space=pltpu.VMEM)
    scratch = [
        pltpu.VMEM((20, 40, 256), F32), pltpu.VMEM((20, 40, 256), F32),
        pltpu.VMEM((20, 1, 256), F32), pltpu.VMEM((20, 1, 256), F32),
        pltpu.VMEM((4, 48, 1024), F32), pltpu.VMEM((4, 1, 512), F32),
        pltpu.VMEM((4, 48, 384), F32), pltpu.VMEM((2, 9, 384), F32),
        pltpu.VMEM((12, 48, 128), F32), pltpu.VMEM((12, 128), F32), pltpu.VMEM((12, 128), F32),
        pltpu.VMEM((12, 40, 128), F32), pltpu.VMEM((12, 40, 128), F32)]

    def body(*refs):
        compute_kernel(n_gx, n_gy, *refs)

    return pl.pallas_call(
        body, out_shape=jax.ShapeDtypeStruct((LEVELS, OWN, 8, 128), F32),
        in_specs=[vmem] * 3, out_specs=vmem, scratch_shapes=scratch, name="analyse", **kw)(gathered, aux, blocks)


def solution(mesh):
    n_gx, n_gy = mesh.shape["gx"], mesh.shape["gy"]
    vmem = pl.BlockSpec(memory_space=pltpu.VMEM)

    def local(*args):
        chunks, aux, blocks = prepare(*args)
        dma = pltpu.SemaphoreType.DMA

        def gather_body(*refs):
            gather_kernel(n_gx, n_gy, *refs)

        gathered, aux_all = pl.pallas_call(
            gather_body,
            out_shape=(jax.ShapeDtypeStruct((3, 3, LEVELS, 80, 128), F32), jax.ShapeDtypeStruct((3, 3, AUX, 128), F32)),
            in_specs=[vmem] * 2, out_specs=(vmem, vmem),
            scratch_shapes=[dma((3, LEVELS)), dma((3, LEVELS)), dma((3,)), dma((3,)),
                            dma((2, 3, LEVELS + 1)), dma((2, 3, LEVELS + 1)), dma((2,))],
            compiler_params=pltpu.CompilerParams(collective_id=0, has_side_effects=True),
            name="gather")(chunks, aux)
        analysed = compute_call(n_gx, n_gy, gathered, aux_all, blocks)
        out = pl.pallas_call(
            return_kernel, out_shape=jax.ShapeDtypeStruct((LEVELS, OWN, 8, 128), F32),
            in_specs=[vmem], out_specs=vmem,
            scratch_shapes=[dma((LEVELS,)), dma((LEVELS,)), dma((1,))],
            compiler_params=pltpu.CompilerParams(collective_id=1, has_side_effects=True),
            name="give_back")(analysed)
        return out.transpose(1, 0, 2, 3)

    return jax.shard_map(
        local,
        mesh=mesh,
        in_specs=(
            P("mem", None, "gx", "gy"),
            P(None, "gx", "gy"),
            P("gx", "gy"),
            P(None, None, "gx", "gy"),
            P(None, None, "gx", "gy"),
            P(None, None, "gx", "gy"),
            P(None, "gx", "gy"),
        ),
        out_specs=P("mem", None, "gx", "gy"),
        check_vma=False,
    )
```

profile of v0, /device:TPU:32, one launch (start us, length us, event | category | flops | bytes accessed | tf_op | source)
XLA Modules:
  0.0 73.6 jit_solution(4782143174041740006)
XLA Ops:
  0.0 0.0 copy-start
  0.0 0.8 %constant_dynamic-slice_fusion = (f32[1,16,2,16]{3,2,1,0:T(2,128)S(1)}, f32[1,16,2,16]{3,2,1,0:T(2,128)S(1)}) fusion(f32[4,16,2,16]{3,2,1,0:T(2,128)} %param.11, s32[]{:T(128)S(6)} %select_n.9, f32[4,16,2,16]{3,2,1,0:T(2,128)} %param.10), kind=kLoop, calls=%fused_computation.7 | loop fusion | bytes 8196 | tf_op jit(solution)/shard_map/jit(dynamic_index_in_dim)/dynamic_slice | solution.py:374
  0.8 0.1 copy.33
  0.8 0.1 stack_reshape.10
  0.9 0.1 copy.32
  1.0 0.1 stack_reshape.9
  1.1 0.7 convert_bitcast_fusion
  1.8 0.1 copy.27
  1.9 0.1 stack_reshape.11
  2.0 0.0 copy-done
  2.0 0.7 convert_element_type.9
  2.7 0.1 pad.3.clone
  2.8 0.7 maximum_maximum_fusion.refs_1_
  3.5 0.9 %slice.17 = f32[4,6,8,128]{3,1,0,2:T(8,128)S(1)} slice(f32[4,8,10,128]{3,1,0,2:T(8,128)} %bitcast.27), slice={[0:4], [2:8], [0:8], [0:128]} | slice | bytes 196608 | tf_op jit(solution)/shard_map/slice | solution.py:370
  4.4 0.1 copy.36
  4.5 0.8 %slice.16 = f32[4,8,2,128]{3,1,0,2:T(8,128)S(1)} slice(f32[4,8,10,128]{3,1,0,2:T(8,128)} %bitcast.28), slice={[0:4], [0:8], [8:10], [0:128]} | slice | bytes 65536 | tf_op jit(solution)/shard_map/slice | solution.py:369
  5.3 0.9 %slice.15 = f32[4,2,8,128]{3,1,0,2:T(2,128)S(1)} slice(f32[4,8,10,128]{3,1,0,2:T(8,128)} %bitcast.29), slice={[0:4], [0:2], [0:8], [0:128]} | slice | bytes 65536 | tf_op jit(solution)/shard_map/slice | solution.py:369
  6.2 0.7 pad_maximum_fusion.refs_0_
  6.9 41.4 %gather.1 = (f32[3,3,4,80,128]{4,3,2,1,0:T(8,128)}, f32[3,3,32,128]{3,2,1,0:T(8,128)}) custom-call(f32[4,80,128]{2,1,0:T(8,128)} %pad_maximum_fusion.refs_0_, f32[32,128]{1,0:T(8,128)} %maximum_maximum_fusion.refs_1_), custom_call_target="tpu_custom_call" | custom-call | tf_op jit(solution)/shard_map/gather/pallas_call | solution.py:414
  48.3 0.1 broadcast_in_dim.10
  48.4 0.7 reshape.21.refs_2_
  49.1 14.3 %analyse.1.y_ref = f32[4,10,8,128]{3,2,1,0:T(8,128)} custom-call(f32[3,3,4,80,128]{4,3,2,1,0:T(8,128)} %get-tuple-element.7.refs_0_, f32[3,3,32,128]{3,2,1,0:T(8,128)} %get-tuple-element.8.refs_1_, s32[20,128]{1,0:T(8,128)} %reshape.21.refs_2_), custom_call_target="tpu_custom_call" | custom-call | tf_op jit(solution)/shard_map/analyse/pallas_call | solution.py:398
  63.4 8.6 %give_back.1 = f32[4,10,8,128]{3,2,1,0:T(8,128)} custom-call(f32[4,10,8,128]{3,2,1,0:T(8,128)} %analyse.1.y_ref), custom_call_target="tpu_custom_call" | custom-call | tf_op jit(solution)/shard_map/give_back/pallas_call | solution.py:423
  72.0 1.6 %copy.29 = f32[10,4,8,128]{3,2,1,0:T(8,128)} copy(f32[10,4,8,128]{3,2,0,1:T(8,128)} %bitcast.25) | data formatting | bytes 327680 | tf_op jit(solution)/shard_map/transpose | solution.py:429
  (9 shorter events, 0.1 us)
Async XLA Ops:
  0.0 2.0 %copy-start = (f32[4,8,128]{2,1,0:T(8,128)S(1)}, f32[4,8,128]{2,1,0:T(8,128)}, u32[]{:S(2)}) copy-start(f32[4,8,128]{2,1,0:T(8,128)} %param.8) | copy-start | bytes 49156
  0.0 48.3 %copy-start.1 = (s32[5,2,16]{2,1,0:T(2,128)S(1)}, s32[5,2,16]{2,1,0:T(2,128)}, u32[]{:S(2)}) copy-start(s32[5,2,16]{2,1,0:T(2,128)} %param.13) | copy-start | bytes 1924
where the time goes:
time: 74.1 us; the launch traced here: 73.6 us
  Pallas kernels  64.3 us (87%)
  local copies, waits for them, and re-layouts  6.42 us (9%)
  other arithmetic  2.78 us (4%)
    pallas_call x1, Pallas kernels, local(): pl.pallas_call(gather_body, out_shape=(jax.ShapeDtypeStruct((3, 3, LEVELS...  41.4 us
    pallas_call x1, Pallas kernels, compute_call(): pl.pallas_call(body, out_shape=jax.ShapeDtypeStruct((LEVELS, OWN, 8, 128)...  14.3 us
    pallas_call x1, Pallas kernels, local(): pl.pallas_call(return_kernel, out_shape=jax.ShapeDtypeStruct((LEVELS, OWN...  8.56 us
    transpose x1, local copies, waits for them, and re-layouts, local(): return out.transpose(1, 0, 2, 3)  1.6 us

commit v1 on v0

--- a/solution.py
+++ b/solution.py
@@ -16,12 +16,44 @@
 NEED = ((16, 64), (0, 80), (0, 64))
 
 
-def gather_kernel(n_gx, n_gy, x_ref, aux_ref, g_ref, a_ref, ssem, rsem, asem, arsem, fsem, frsem, lsem):
+def neighbours(n_gx, n_gy):
     mem, gx, gy = lax.axis_index("mem"), lax.axis_index("gx"), lax.axis_index("gy")
     rows = (lax.rem(gx + n_gx - 1, n_gx), gx, lax.rem(gx + 1, n_gx))
     sides = (lax.rem(gy + n_gy - 1, n_gy), lax.rem(gy + 1, n_gy))
     there = [lax.rem(mem + o, LEVELS) for o in range(LEVELS)]
     back = [lax.rem(mem + LEVELS - o, LEVELS) for o in range(LEVELS)]
+    return mem, gx, gy, rows, sides, there, back
+
+
+def prepare(level, x_ref, dif_ref, mask_ref, val_ref, var_ref, cell_ref, blk_ref, xs, aux, ob):
+    flat = x_ref.reshape(OWN * LEVELS * 8, 128)
+    for k in range(LEVELS):
+        for r in range(8):
+            main = 8 * r if r < 2 else 16 + 8 * r
+            xs[k, main:main + 8, :] = flat[pl.ds(k * 8 + r, 8, stride=32), :]
+            xs[k, 16 + 2 * r:18 + 2 * r, :] = flat[pl.ds(256 + k * 8 + r, 2, stride=32), :]
+    aux[0:8, :] = dif_ref[level]
+    aux[8:16, :] = mask_ref[...].astype(F32)
+    spread_out = jnp.where(iota((16, 256), 0) == iota((16, 256), 1) >> 4, 1.0, 0.0).astype(F32)
+    kinds = [ref[level].astype(F32) for ref in (val_ref, var_ref, cell_ref)]
+    stacked = jnp.concatenate([kinds[k][:, a, :] for a in range(2) for k in range(3)], axis=0)
+    wide = lax.dot_general(stacked, spread_out, (((1,), (0,)), ((), ())), precision=lax.Precision.HIGHEST,
+                           preferred_element_type=F32)
+    mine = iota((16, 256), 0) == (iota((16, 256), 1) & 15)
+    for n in range(6):
+        row = jnp.sum(jnp.where(mine, wide[16 * n:16 * n + 16], 0.0), axis=0, keepdims=True)
+        aux[16 + 2 * n:17 + 2 * n, :] = row[:, 0:128]
+        aux[17 + 2 * n:18 + 2 * n, :] = row[:, 128:256]
+    aux[28:32, :] = jnp.zeros((4, 128), F32)
+    blocks = blk_ref[...].astype(F32)
+    blocks = jnp.concatenate([blocks[:, a, :] for a in range(2)] + [jnp.zeros((6, 16), F32)], axis=0)
+    ob[...] = mxu(blocks, spread_out)
+
+
+def cycle_kernel(n_gx, n_gy, x_any, dif_any, mask_any, val_any, var_any, cell_any, blk_any, out_ref,
+                 x_ref, dif_ref, mask_ref, val_ref, var_ref, cell_ref, blk_ref, xs, aux, ob, g_ref, a_ref, y_ref, *rest):
+    scratch, (ssem, rsem, asem, arsem, fsem, frsem, lsem, bsem, brsem) = rest[:-9], rest[-9:]
+    mem, gx, gy, rows, sides, there, back = neighbours(n_gx, n_gy)
 
     barrier = pltpu.get_barrier_semaphore()
     count = 0
@@ -35,10 +67,14 @@
         pl.semaphore_signal(barrier, inc=1, device_id=(mem, gx, side), device_id_type=MESH)
         count += 1
 
-    own = pltpu.make_async_copy(x_ref.at[mem], g_ref.at[1, 1, mem], lsem.at[0])
-    own_aux = pltpu.make_async_copy(aux_ref, a_ref.at[1, 1], lsem.at[1])
-    own.start()
-    own_aux.start()
+    loads = [pltpu.make_async_copy(src, dst, lsem.at[n]) for n, (src, dst) in enumerate((
+        (x_any, x_ref), (dif_any, dif_ref), (mask_any, mask_ref), (val_any, val_ref), (var_any, var_ref),
+        (cell_any, cell_ref), (blk_any, blk_ref)))]
+    for load in loads:
+        load.start()
+    for load in loads:
+        load.wait()
+    prepare(mem, x_ref, dif_ref, mask_ref, val_ref, var_ref, cell_ref, blk_ref, xs, aux, ob)
     pl.semaphore_wait(barrier, count)
 
     sends = []
@@ -56,7 +92,7 @@
     def scatter(d, o):
         part = pl.ds(*NEED[2 - d])
         copy = pltpu.make_async_remote_copy(
-            src_ref=x_ref.at[there[o], part], dst_ref=g_ref.at[1, 2 - d, mem, part],
+            src_ref=xs.at[there[o], part], dst_ref=g_ref.at[1, 2 - d, mem, part],
             send_sem=ssem.at[d, o], recv_sem=rsem.at[2 - d, o],
             device_id=(there[o], rows[d], gy), device_id_type=MESH)
         copy.start()
@@ -64,7 +100,7 @@
 
     for d in (0, 2):
         copy = pltpu.make_async_remote_copy(
-            src_ref=aux_ref, dst_ref=a_ref.at[1, 2 - d], send_sem=asem.at[d], recv_sem=arsem.at[2 - d],
+            src_ref=aux, dst_ref=a_ref.at[1, 2 - d], send_sem=asem.at[d], recv_sem=arsem.at[2 - d],
             device_id=(mem, rows[d], gy), device_id_type=MESH)
         copy.start()
         sends.append(copy)
@@ -73,44 +109,57 @@
         scatter(2, o)
     for o in range(1, LEVELS):
         scatter(1, o)
-    forward(aux_ref, 1, None, None, LEVELS)
-    forward(x_ref.at[mem], 1, mem, pl.ds(0, 80), 0)
-
-    def arrival(dg, o, source):
+    forward(aux, 1, None, None, LEVELS)
+    forward(xs.at[mem], 1, mem, pl.ds(0, 80), 0)
+    g_ref[1, 1, mem] = xs[mem]
+    a_ref[1, 1] = aux[...]
+
+    def arrival(dg, o):
         part = pl.ds(*NEED[dg])
-        return pltpu.make_async_remote_copy(
-            src_ref=x_ref.at[0, part], dst_ref=g_ref.at[1, dg, source, part],
+        pltpu.make_async_remote_copy(
+            src_ref=xs.at[0, part], dst_ref=g_ref.at[1, dg, back[o], part],
             send_sem=ssem.at[dg, o], recv_sem=rsem.at[dg, o],
-            device_id=(mem, rows[dg], gy), device_id_type=MESH)
-
-    for dg, o in [(1, 1), (1, 3), (1, 2)]:
-        arrival(dg, o, back[o]).wait_recv()
-        forward(g_ref.at[1, dg, back[o], pl.ds(*NEED[dg])], dg, back[o], pl.ds(*NEED[dg]), o)
+            device_id=(mem, rows[dg], gy), device_id_type=MESH).wait_recv()
+        forward(g_ref.at[1, dg, back[o], part], dg, back[o], part, o)
+
+    for o in (1, 3, 2):
+        arrival(1, o)
     for dg in (0, 2):
         pltpu.make_async_remote_copy(
-            src_ref=aux_ref, dst_ref=a_ref.at[1, dg], send_sem=asem.at[dg], recv_sem=arsem.at[dg],
+            src_ref=aux, dst_ref=a_ref.at[1, dg], send_sem=asem.at[dg], recv_sem=arsem.at[dg],
             device_id=(mem, rows[dg], gy), device_id_type=MESH).wait_recv()
         forward(a_ref.at[1, dg], dg, None, None, LEVELS)
     for o in range(LEVELS):
         for dg in (0, 2):
-            arrival(dg, o, back[o]).wait_recv()
-            forward(g_ref.at[1, dg, back[o], pl.ds(*NEED[dg])], dg, back[o], pl.ds(*NEED[dg]), o)
+            arrival(dg, o)
     for h in (0, 2):
         for dg in range(3):
             for o in range(LEVELS):
                 part = pl.ds(*NEED[dg])
                 pltpu.make_async_remote_copy(
-                    src_ref=x_ref.at[0, part], dst_ref=g_ref.at[h, dg, back[o], part],
+                    src_ref=xs.at[0, part], dst_ref=g_ref.at[h, dg, back[o], part],
                     send_sem=fsem.at[0, dg, o], recv_sem=frsem.at[h // 2, dg, o],
                     device_id=(mem, gx, sides[0]), device_id_type=MESH).wait_recv()
             pltpu.make_async_remote_copy(
-                src_ref=aux_ref, dst_ref=a_ref.at[h, dg],
+                src_ref=aux, dst_ref=a_ref.at[h, dg],
                 send_sem=fsem.at[0, dg, LEVELS], recv_sem=frsem.at[h // 2, dg, LEVELS],
                 device_id=(mem, gx, sides[0]), device_id_type=MESH).wait_recv()
+
+    compute_kernel(n_gx, n_gy, g_ref, a_ref, ob, y_ref, *scratch)
+
+    for o in range(1, LEVELS):
+        copy = pltpu.make_async_remote_copy(
+            src_ref=y_ref.at[there[o]], dst_ref=out_ref.at[:, mem], send_sem=bsem.at[o], recv_sem=brsem.at[o],
+            device_id=(there[o], gx, gy), device_id_type=MESH)
+        copy.start()
+        sends.append(copy)
+    out_ref[:, mem] = y_ref[mem]
+    for o in range(1, LEVELS):
+        pltpu.make_async_remote_copy(
+            src_ref=y_ref.at[0], dst_ref=out_ref.at[:, back[o]], send_sem=bsem.at[o], recv_sem=brsem.at[o],
+            device_id=(there[o], gx, gy), device_id_type=MESH).wait_recv()
     for copy in sends:
         copy.wait_send()
-    own.wait()
-    own_aux.wait()
 
 
 def split(x):
@@ -236,8 +285,7 @@
                 taper = 1.0 if code == 4 else 0.5 if (r == 1 or c == 1) else 0.25
                 chosen = jnp.zeros((1, 256), F32)
                 for s in range(5):
-                    at = (s * 2 + a) * 2
-                    blocks = jnp.concatenate([ob_ref[at:at + 1, :], ob_ref[at + 1:at + 2, :]], axis=1)
+                    blocks = ob_ref[5 * a + s:5 * a + s + 1, :]
                     chosen = chosen + jnp.where(blocks == code, taper, 0.0)
                 chosen = jnp.concatenate([chosen, jnp.zeros((1, 128), F32)], axis=1)
                 near.append(pltpu.roll(chosen, (16 * (c - 1)) % 384, 1) if c != 1 else chosen)
@@ -324,11 +372,12 @@
             low = three_high_by(plow, patch, 3 * g)
             total = total + mxu(jnp.concatenate([th, tl, th], axis=1), jnp.concatenate([high, high, low], axis=0))
         total = total + mean[a + 1]
+        flat = out_ref.reshape(MEMBERS * 8, 128)
         for r in range(4):
             value = total[:, 128 * r:128 * r + 128]
             for s in range(LEVELS):
-                out_ref[s, 0:8, 4 * a + r, :] = value[8 * s:8 * s + 8]
-                out_ref[s, 8:10, 4 * a + r, :] = value[32 + 2 * s:34 + 2 * s]
+                flat[pl.ds(80 * s + 4 * a + r, 8, stride=8), :] = value[8 * s:8 * s + 8]
+                flat[pl.ds(80 * s + 64 + 4 * a + r, 2, stride=8), :] = value[32 + 2 * s:34 + 2 * s]
 
 
 def three_high_by(value, patch, first):
@@ -336,55 +385,8 @@
     return jnp.concatenate(parts + [jnp.zeros((8, value.shape[1]), F32)], axis=0)
 
 
-def return_kernel(y_ref, out_ref, ssem, rsem, lsem):
-    mem, gx, gy = lax.axis_index("mem"), lax.axis_index("gx"), lax.axis_index("gy")
-    there = [lax.rem(mem + o, LEVELS) for o in range(LEVELS)]
-    back = [lax.rem(mem + LEVELS - o, LEVELS) for o in range(LEVELS)]
-    barrier = pltpu.get_barrier_semaphore()
-    for o in range(1, LEVELS):
-        pl.semaphore_signal(barrier, inc=1, device_id=(there[o], gx, gy), device_id_type=MESH)
-    own = pltpu.make_async_copy(y_ref.at[mem], out_ref.at[mem], lsem.at[0])
-    own.start()
-    pl.semaphore_wait(barrier, LEVELS - 1)
-    sends = []
-    for o in range(1, LEVELS):
-        copy = pltpu.make_async_remote_copy(
-            src_ref=y_ref.at[there[o]], dst_ref=out_ref.at[mem], send_sem=ssem.at[o], recv_sem=rsem.at[o],
-            device_id=(there[o], gx, gy), device_id_type=MESH)
-        copy.start()
-        sends.append(copy)
-    for o in range(1, LEVELS):
-        pltpu.make_async_remote_copy(
-            src_ref=y_ref.at[0], dst_ref=out_ref.at[back[o]], send_sem=ssem.at[o], recv_sem=rsem.at[o],
-            device_id=(there[o], gx, gy), device_id_type=MESH).wait_recv()
-    for copy in sends:
-        copy.wait_send()
-    own.wait()
-
-
-def prepare(initial_states, diffusivity, ocean_mask, obs_values, obs_variance, obs_cells, obs_blocks):
-    x = initial_states.transpose(1, 2, 0, 3)
-    main = x[:, :, :8]
-    chunks = jnp.concatenate([
-        main[:, :2].reshape(LEVELS, 16, 128), x[:, :, 8:].reshape(LEVELS, 16, 128),
-        main[:, 2:].reshape(LEVELS, 48, 128)], axis=1)
-    level = lax.axis_index("mem")
-
-    def lanes(v):
-        v = lax.dynamic_index_in_dim(v, level, 0, keepdims=False).astype(F32)
-        return v.transpose(1, 2, 0).reshape(2, 2, 128)
-
-    obs = jnp.stack([lanes(obs_values), lanes(obs_variance), lanes(obs_cells)], axis=1).reshape(12, 128)
-    aux = jnp.concatenate([
-        lax.dynamic_index_in_dim(diffusivity, level, 0, keepdims=False), ocean_mask.astype(F32), obs,
-        jnp.zeros((4, 128), F32)], axis=0)
-    blocks = jnp.broadcast_to(obs_blocks[:, :, :, None], obs_blocks.shape + (OBS,)).reshape(20, 128)
-    return chunks, aux, blocks
-
-
-def compute_call(n_gx, n_gy, gathered, aux, blocks, **kw):
-    vmem = pl.BlockSpec(memory_space=pltpu.VMEM)
-    scratch = [
+def scratch_of():
+    return [
         pltpu.VMEM((20, 40, 256), F32), pltpu.VMEM((20, 40, 256), F32),
         pltpu.VMEM((20, 1, 256), F32), pltpu.VMEM((20, 1, 256), F32),
         pltpu.VMEM((4, 48, 1024), F32), pltpu.VMEM((4, 1, 512), F32),
@@ -392,41 +394,26 @@
         pltpu.VMEM((12, 48, 128), F32), pltpu.VMEM((12, 128), F32), pltpu.VMEM((12, 128), F32),
         pltpu.VMEM((12, 40, 128), F32), pltpu.VMEM((12, 40, 128), F32)]
 
-    def body(*refs):
-        compute_kernel(n_gx, n_gy, *refs)
-
-    return pl.pallas_call(
-        body, out_shape=jax.ShapeDtypeStruct((LEVELS, OWN, 8, 128), F32),
-        in_specs=[vmem] * 3, out_specs=vmem, scratch_shapes=scratch, name="analyse", **kw)(gathered, aux, blocks)
-
 
 def solution(mesh):
     n_gx, n_gy = mesh.shape["gx"], mesh.shape["gy"]
-    vmem = pl.BlockSpec(memory_space=pltpu.VMEM)
+    dma = pltpu.SemaphoreType.DMA
 
     def local(*args):
-        chunks, aux, blocks = prepare(*args)
-        dma = pltpu.SemaphoreType.DMA
-
-        def gather_body(*refs):
-            gather_kernel(n_gx, n_gy, *refs)
-
-        gathered, aux_all = pl.pallas_call(
-            gather_body,
-            out_shape=(jax.ShapeDtypeStruct((3, 3, LEVELS, 80, 128), F32), jax.ShapeDtypeStruct((3, 3, AUX, 128), F32)),
-            in_specs=[vmem] * 2, out_specs=(vmem, vmem),
-            scratch_shapes=[dma((3, LEVELS)), dma((3, LEVELS)), dma((3,)), dma((3,)),
-                            dma((2, 3, LEVELS + 1)), dma((2, 3, LEVELS + 1)), dma((2,))],
+        def body(*refs):
+            cycle_kernel(n_gx, n_gy, *refs)
+
+        return pl.pallas_call(
+            body, out_shape=jax.ShapeDtypeStruct((OWN, LEVELS, 8, 128), F32),
+            in_specs=[pl.BlockSpec(memory_space=pl.ANY)] * 7, out_specs=pl.BlockSpec(memory_space=pltpu.VMEM),
+            scratch_shapes=[pltpu.VMEM(a.shape, a.dtype) for a in args] + [
+                pltpu.VMEM((LEVELS, 80, 128), F32), pltpu.VMEM((AUX, 128), F32), pltpu.VMEM((16, 256), F32),
+                pltpu.VMEM((3, 3, LEVELS, 80, 128), F32), pltpu.VMEM((3, 3, AUX, 128), F32),
+                pltpu.VMEM((LEVELS, OWN, 8, 128), F32)] + scratch_of() + [
+                dma((3, LEVELS)), dma((3, LEVELS)), dma((3,)), dma((3,)),
+                dma((2, 3, LEVELS + 1)), dma((2, 3, LEVELS + 1)), dma((7,)), dma((LEVELS,)), dma((LEVELS,))],
             compiler_params=pltpu.CompilerParams(collective_id=0, has_side_effects=True),
-            name="gather")(chunks, aux)
-        analysed = compute_call(n_gx, n_gy, gathered, aux_all, blocks)
-        out = pl.pallas_call(
-            return_kernel, out_shape=jax.ShapeDtypeStruct((LEVELS, OWN, 8, 128), F32),
-            in_specs=[vmem], out_specs=vmem,
-            scratch_shapes=[dma((LEVELS,)), dma((LEVELS,)), dma((1,))],
-            compiler_params=pltpu.CompilerParams(collective_id=1, has_side_effects=True),
-            name="give_back")(analysed)
-        return out.transpose(1, 0, 2, 3)
+            name="cycle")(*args)
 
     return jax.shard_map(
         local,

time: 74.1 us -> 59.5 us (0.80)
  the two profiles are of different devices: /device:TPU:32 before, /device:TPU:1 now
where the time goes in v1:
time: 59.5 us; the launch traced here: 59.3 us
  Pallas kernels  57.7 us (97%)
  local copies, waits for them, and re-layouts  1.59 us (3%)
    pallas_call x1, Pallas kernels, local(): pl.pallas_call(body, out_shape=jax.ShapeDtypeStruct((OWN, LEVELS, 8, 128)...  57.7 us
    unnamed x1, local copies, waits for them, and re-layouts  1.59 us

profile of v1, /device:TPU:1, one launch (start us, length us, event | category | flops | bytes accessed | tf_op | source)
XLA Modules:
  0.0 59.3 jit_solution(9231516846301593013)
XLA Ops:
  0.0 57.7 %cycle.1 = f32[10,4,8,128]{3,2,1,0:T(8,128)} custom-call(f32[10,4,8,128]{3,2,1,0:T(8,128)} %refs_0_.1, f32[4,8,128]{2,1,0:T(8,128)} %refs_1_.1, s32[8,128]{1,0:T(8,128)} %refs_2_.1, f32[4,16,2,16]{3,2,1,0:T(2,128)} %refs_3_.1, f32[4,16,2,16]{3,2,1,0:T(2,128)} %refs_4_.1, s32[4,16,2,16]{3,2,1,0:T(2,128)} %refs_5_.1, s32[5,2,16]{2,1,0:T(2,128)} %refs_6_.1), custom_call_target="tpu_custom_call" | custom-call | tf_op jit(solution)/shard_map/cycle/pallas_call | solution.py:406
  57.7 1.6 %copy.9 = f32[10,4,8,128]{3,2,1,0:T(8,128)} copy(f32[10,4,8,128]{3,2,1,0:T(8,128)} %cycle.1) | data formatting | bytes 327680

commit v2 on v1

--- a/solution.py
+++ b/solution.py
@@ -55,17 +55,29 @@
     scratch, (ssem, rsem, asem, arsem, fsem, frsem, lsem, bsem, brsem) = rest[:-9], rest[-9:]
     mem, gx, gy, rows, sides, there, back = neighbours(n_gx, n_gy)
 
+    in_rows = (gx > 0, None, gx < n_gx - 1)
+    in_sides = (gy > 0, gy < n_gy - 1)
+
+    def when(*conditions):
+        known = [c for c in conditions if c is not None]
+        if not known:
+            return lambda f: f()
+        return pl.when(known[0] if len(known) == 1 else known[0] & known[1])
+
     barrier = pltpu.get_barrier_semaphore()
-    count = 0
+    count = LEVELS - 1
     for d in range(3):
-        for o in range(LEVELS):
-            if d == 1 and o == 0:
-                continue
-            pl.semaphore_signal(barrier, inc=1, device_id=(there[o], rows[d], gy), device_id_type=MESH)
-            count += 1
-    for side in sides:
-        pl.semaphore_signal(barrier, inc=1, device_id=(mem, gx, side), device_id_type=MESH)
-        count += 1
+        @when(in_rows[d])
+        def _():
+            for o in range(1 if d == 1 else 0, LEVELS):
+                pl.semaphore_signal(barrier, inc=1, device_id=(there[o], rows[d], gy), device_id_type=MESH)
+        if d != 1:
+            count = count + jnp.where(in_rows[d], LEVELS, 0)
+    for e in range(2):
+        @when(in_sides[e])
+        def _():
+            pl.semaphore_signal(barrier, inc=1, device_id=(mem, gx, sides[e]), device_id_type=MESH)
+        count = count + jnp.where(in_sides[e], 1, 0)
 
     loads = [pltpu.make_async_copy(src, dst, lsem.at[n]) for n, (src, dst) in enumerate((
         (x_any, x_ref), (dif_any, dif_ref), (mask_any, mask_ref), (val_any, val_ref), (var_any, var_ref),
@@ -75,91 +87,108 @@
     for load in loads:
         load.wait()
     prepare(mem, x_ref, dif_ref, mask_ref, val_ref, var_ref, cell_ref, blk_ref, xs, aux, ob)
+    for dg in (0, 2):
+        @when(~in_rows[dg])
+        def _():
+            for h in range(3):
+                g_ref[h, dg] = jnp.zeros((LEVELS, 80, 128), F32)
+                a_ref[h, dg] = jnp.ones((AUX, 128), F32)
+    for h in (0, 2):
+        @when(~in_sides[h // 2])
+        def _():
+            g_ref[h] = jnp.zeros((3, LEVELS, 80, 128), F32)
+            a_ref[h] = jnp.ones((3, AUX, 128), F32)
     pl.semaphore_wait(barrier, count)
 
     sends = []
+
+    def start(copy, *conditions):
+        when(*conditions)(copy.start)
+        sends.append((copy, conditions))
 
     def forward(source, dg, slot, part, index):
         for e, side in enumerate(sides):
             h = 2 if e == 0 else 0
             dst = a_ref.at[h, dg] if slot is None else g_ref.at[h, dg, slot, part]
-            copy = pltpu.make_async_remote_copy(
+            start(pltpu.make_async_remote_copy(
                 src_ref=source, dst_ref=dst, send_sem=fsem.at[e, dg, index], recv_sem=frsem.at[h // 2, dg, index],
-                device_id=(mem, gx, side), device_id_type=MESH)
-            copy.start()
-            sends.append(copy)
+                device_id=(mem, gx, side), device_id_type=MESH), in_rows[dg], in_sides[e])
 
     def scatter(d, o):
         part = pl.ds(*NEED[2 - d])
-        copy = pltpu.make_async_remote_copy(
+        start(pltpu.make_async_remote_copy(
             src_ref=xs.at[there[o], part], dst_ref=g_ref.at[1, 2 - d, mem, part],
             send_sem=ssem.at[d, o], recv_sem=rsem.at[2 - d, o],
-            device_id=(there[o], rows[d], gy), device_id_type=MESH)
-        copy.start()
-        sends.append(copy)
-
+            device_id=(there[o], rows[d], gy), device_id_type=MESH), in_rows[d])
+
+    def scatter_aux(d):
+        start(pltpu.make_async_remote_copy(
+            src_ref=aux, dst_ref=a_ref.at[1, 2 - d], send_sem=asem.at[d], recv_sem=arsem.at[2 - d],
+            device_id=(mem, rows[d], gy), device_id_type=MESH), in_rows[d])
+
+    forward(aux, 1, None, None, LEVELS)
+    forward(xs.at[mem], 1, mem, pl.ds(0, 80), 0)
+    for o in range(1, LEVELS):
+        scatter(1, o)
     for d in (0, 2):
-        copy = pltpu.make_async_remote_copy(
-            src_ref=aux, dst_ref=a_ref.at[1, 2 - d], send_sem=asem.at[d], recv_sem=arsem.at[2 - d],
-            device_id=(mem, rows[d], gy), device_id_type=MESH)
-        copy.start()
-        sends.append(copy)
+        scatter_aux(d)
     for o in range(LEVELS):
         scatter(0, o)
         scatter(2, o)
-    for o in range(1, LEVELS):
-        scatter(1, o)
-    forward(aux, 1, None, None, LEVELS)
-    forward(xs.at[mem], 1, mem, pl.ds(0, 80), 0)
     g_ref[1, 1, mem] = xs[mem]
     a_ref[1, 1] = aux[...]
 
     def arrival(dg, o):
         part = pl.ds(*NEED[dg])
-        pltpu.make_async_remote_copy(
-            src_ref=xs.at[0, part], dst_ref=g_ref.at[1, dg, back[o], part],
-            send_sem=ssem.at[dg, o], recv_sem=rsem.at[dg, o],
-            device_id=(mem, rows[dg], gy), device_id_type=MESH).wait_recv()
+
+        @when(in_rows[dg])
+        def _():
+            pltpu.make_async_remote_copy(
+                src_ref=xs.at[0, part], dst_ref=g_ref.at[1, dg, back[o], part],
+                send_sem=ssem.at[dg, o], recv_sem=rsem.at[dg, o],
+                device_id=(mem, rows[dg], gy), device_id_type=MESH).wait_recv()
         forward(g_ref.at[1, dg, back[o], part], dg, back[o], part, o)
 
     for o in (1, 3, 2):
         arrival(1, o)
     for dg in (0, 2):
-        pltpu.make_async_remote_copy(
-            src_ref=aux, dst_ref=a_ref.at[1, dg], send_sem=asem.at[dg], recv_sem=arsem.at[dg],
-            device_id=(mem, rows[dg], gy), device_id_type=MESH).wait_recv()
+        @when(in_rows[dg])
+        def _():
+            pltpu.make_async_remote_copy(
+                src_ref=aux, dst_ref=a_ref.at[1, dg], send_sem=asem.at[dg], recv_sem=arsem.at[dg],
+                device_id=(mem, rows[dg], gy), device_id_type=MESH).wait_recv()
         forward(a_ref.at[1, dg], dg, None, None, LEVELS)
     for o in range(LEVELS):
         for dg in (0, 2):
             arrival(dg, o)
     for h in (0, 2):
-        for dg in range(3):
-            for o in range(LEVELS):
-                part = pl.ds(*NEED[dg])
+        for dg in (1, 0, 2):
+            @when(in_sides[h // 2], in_rows[dg])
+            def _():
+                for o in range(LEVELS):
+                    part = pl.ds(*NEED[dg])
+                    pltpu.make_async_remote_copy(
+                        src_ref=xs.at[0, part], dst_ref=g_ref.at[h, dg, back[o], part],
+                        send_sem=fsem.at[0, dg, o], recv_sem=frsem.at[h // 2, dg, o],
+                        device_id=(mem, gx, sides[0]), device_id_type=MESH).wait_recv()
                 pltpu.make_async_remote_copy(
-                    src_ref=xs.at[0, part], dst_ref=g_ref.at[h, dg, back[o], part],
-                    send_sem=fsem.at[0, dg, o], recv_sem=frsem.at[h // 2, dg, o],
+                    src_ref=aux, dst_ref=a_ref.at[h, dg],
+                    send_sem=fsem.at[0, dg, LEVELS], recv_sem=frsem.at[h // 2, dg, LEVELS],
                     device_id=(mem, gx, sides[0]), device_id_type=MESH).wait_recv()
-            pltpu.make_async_remote_copy(
-                src_ref=aux, dst_ref=a_ref.at[h, dg],
-                send_sem=fsem.at[0, dg, LEVELS], recv_sem=frsem.at[h // 2, dg, LEVELS],
-                device_id=(mem, gx, sides[0]), device_id_type=MESH).wait_recv()
 
     compute_kernel(n_gx, n_gy, g_ref, a_ref, ob, y_ref, *scratch)
 
     for o in range(1, LEVELS):
-        copy = pltpu.make_async_remote_copy(
+        start(pltpu.make_async_remote_copy(
             src_ref=y_ref.at[there[o]], dst_ref=out_ref.at[:, mem], send_sem=bsem.at[o], recv_sem=brsem.at[o],
-            device_id=(there[o], gx, gy), device_id_type=MESH)
-        copy.start()
-        sends.append(copy)
+            device_id=(there[o], gx, gy), device_id_type=MESH))
     out_ref[:, mem] = y_ref[mem]
     for o in range(1, LEVELS):
         pltpu.make_async_remote_copy(
             src_ref=y_ref.at[0], dst_ref=out_ref.at[:, back[o]], send_sem=bsem.at[o], recv_sem=brsem.at[o],
             device_id=(there[o], gx, gy), device_id_type=MESH).wait_recv()
-    for copy in sends:
-        copy.wait_send()
+    for copy, conditions in sends:
+        when(*conditions)(copy.wait_send)
 
 
 def split(x):

time: 59.5 us -> 55.6 us (0.934)
  the two profiles are of different devices: /device:TPU:1 before, /device:TPU:9 now
where the time goes in v2:
time: 55.6 us; the launch traced here: 55.4 us
  Pallas kernels  53.8 us (97%)
  local copies, waits for them, and re-layouts  1.59 us (3%)
    pallas_call x1, Pallas kernels, local(): pl.pallas_call(body, out_shape=jax.ShapeDtypeStruct((OWN, LEVELS, 8, 128)...  53.8 us
    unnamed x1, local copies, waits for them, and re-layouts  1.59 us

profile of v2, /device:TPU:9, one launch (start us, length us, event | category | flops | bytes accessed | tf_op | source)
XLA Modules:
  0.0 55.4 jit_solution(9863995353064511068)
XLA Ops:
  0.0 53.8 %cycle.1 = f32[10,4,8,128]{3,2,1,0:T(8,128)} custom-call(f32[10,4,8,128]{3,2,1,0:T(8,128)} %refs_0_.1, f32[4,8,128]{2,1,0:T(8,128)} %refs_1_.1, s32[8,128]{1,0:T(8,128)} %refs_2_.1, f32[4,16,2,16]{3,2,1,0:T(2,128)} %refs_3_.1, f32[4,16,2,16]{3,2,1,0:T(2,128)} %refs_4_.1, s32[4,16,2,16]{3,2,1,0:T(2,128)} %refs_5_.1, s32[5,2,16]{2,1,0:T(2,128)} %refs_6_.1), custom_call_target="tpu_custom_call" | custom-call | tf_op jit(solution)/shard_map/cycle/pallas_call | solution.py:435
  53.9 1.6 %copy.9 = f32[10,4,8,128]{3,2,1,0:T(8,128)} copy(f32[10,4,8,128]{3,2,1,0:T(8,128)} %cycle.1) | data formatting | bytes 327680

commit v3 on v2

--- a/solution.py
+++ b/solution.py
@@ -8,6 +8,7 @@
 MESH = pl.DeviceIdType.MESH
 F32 = jnp.float32
 NS_ITERS = 7
+BY_ROWS = (False, False, False)
 LEVELS = 4
 OWN = 10
 MEMBERS = 40
@@ -69,10 +70,10 @@
     for d in range(3):
         @when(in_rows[d])
         def _():
-            for o in range(1 if d == 1 else 0, LEVELS):
+            for o in range(1, LEVELS) if d == 1 else (0,):
                 pl.semaphore_signal(barrier, inc=1, device_id=(there[o], rows[d], gy), device_id_type=MESH)
         if d != 1:
-            count = count + jnp.where(in_rows[d], LEVELS, 0)
+            count = count + jnp.where(in_rows[d], 1, 0)
     for e in range(2):
         @when(in_sides[e])
         def _():
@@ -87,6 +88,8 @@
     for load in loads:
         load.wait()
     prepare(mem, x_ref, dif_ref, mask_ref, val_ref, var_ref, cell_ref, blk_ref, xs, aux, ob)
+    f0, f1, dif, wet, pt, hot, obs, slab, wc = scratch[:9]
+    grid = masks(n_gx, n_gy)
     for dg in (0, 2):
         @when(~in_rows[dg])
         def _():
@@ -114,12 +117,18 @@
                 src_ref=source, dst_ref=dst, send_sem=fsem.at[e, dg, index], recv_sem=frsem.at[h // 2, dg, index],
                 device_id=(mem, gx, side), device_id_type=MESH), in_rows[dg], in_sides[e])
 
-    def scatter(d, o):
-        part = pl.ds(*NEED[2 - d])
+    def scatter(o):
         start(pltpu.make_async_remote_copy(
-            src_ref=xs.at[there[o], part], dst_ref=g_ref.at[1, 2 - d, mem, part],
-            send_sem=ssem.at[d, o], recv_sem=rsem.at[2 - d, o],
-            device_id=(there[o], rows[d], gy), device_id_type=MESH), in_rows[d])
+            src_ref=xs.at[there[o]], dst_ref=g_ref.at[1, 1, mem], send_sem=ssem.at[1, o], recv_sem=rsem.at[1, o],
+            device_id=(there[o], gx, gy), device_id_type=MESH))
+
+    def halo(source, slot, o):
+        for d in (0, 2):
+            part = pl.ds(*NEED[2 - d])
+            start(pltpu.make_async_remote_copy(
+                src_ref=source.at[part], dst_ref=g_ref.at[1, 2 - d, slot, part],
+                send_sem=ssem.at[d, o], recv_sem=rsem.at[2 - d, o],
+                device_id=(mem, rows[d], gy), device_id_type=MESH), in_rows[d])
 
     def scatter_aux(d):
         start(pltpu.make_async_remote_copy(
@@ -129,12 +138,10 @@
     forward(aux, 1, None, None, LEVELS)
     forward(xs.at[mem], 1, mem, pl.ds(0, 80), 0)
     for o in range(1, LEVELS):
-        scatter(1, o)
+        scatter(o)
+    halo(xs.at[mem], mem, 0)
     for d in (0, 2):
         scatter_aux(d)
-    for o in range(LEVELS):
-        scatter(0, o)
-        scatter(2, o)
     g_ref[1, 1, mem] = xs[mem]
     a_ref[1, 1] = aux[...]
 
@@ -147,6 +154,8 @@
                 src_ref=xs.at[0, part], dst_ref=g_ref.at[1, dg, back[o], part],
                 send_sem=ssem.at[dg, o], recv_sem=rsem.at[dg, o],
                 device_id=(mem, rows[dg], gy), device_id_type=MESH).wait_recv()
+        if dg == 1:
+            halo(g_ref.at[1, 1, back[o]], back[o], o)
         forward(g_ref.at[1, dg, back[o], part], dg, back[o], part, o)
 
     for o in (1, 3, 2):
@@ -158,25 +167,40 @@
                 src_ref=aux, dst_ref=a_ref.at[1, dg], send_sem=asem.at[dg], recv_sem=arsem.at[dg],
                 device_id=(mem, rows[dg], gy), device_id_type=MESH).wait_recv()
         forward(a_ref.at[1, dg], dg, None, None, LEVELS)
-    for o in range(LEVELS):
-        for dg in (0, 2):
-            arrival(dg, o)
-    for h in (0, 2):
-        for dg in (1, 0, 2):
-            @when(in_sides[h // 2], in_rows[dg])
-            def _():
-                for o in range(LEVELS):
-                    part = pl.ds(*NEED[dg])
-                    pltpu.make_async_remote_copy(
-                        src_ref=xs.at[0, part], dst_ref=g_ref.at[h, dg, back[o], part],
-                        send_sem=fsem.at[0, dg, o], recv_sem=frsem.at[h // 2, dg, o],
-                        device_id=(mem, gx, sides[0]), device_id_type=MESH).wait_recv()
+    def passed_on(h, dg, chunks):
+        @when(in_sides[h // 2], in_rows[dg])
+        def _():
+            for o in range(LEVELS) if chunks else ():
+                part = pl.ds(*NEED[dg])
+                pltpu.make_async_remote_copy(
+                    src_ref=xs.at[0, part], dst_ref=g_ref.at[h, dg, back[o], part],
+                    send_sem=fsem.at[0, dg, o], recv_sem=frsem.at[h // 2, dg, o],
+                    device_id=(mem, gx, sides[0]), device_id_type=MESH).wait_recv()
+            if not chunks:
                 pltpu.make_async_remote_copy(
                     src_ref=aux, dst_ref=a_ref.at[h, dg],
                     send_sem=fsem.at[0, dg, LEVELS], recv_sem=frsem.at[h // 2, dg, LEVELS],
                     device_id=(mem, gx, sides[0]), device_id_type=MESH).wait_recv()
 
-    compute_kernel(n_gx, n_gy, g_ref, a_ref, ob, y_ref, *scratch)
+    weigh(ob, wc)
+    for dg in (0, 2):
+        arrival(dg, 0)
+    for h in (0, 2):
+        passed_on(h, 1, True)
+        for dg in (1, 0, 2):
+            passed_on(h, dg, False)
+    assemble(grid, g_ref, a_ref, f0, dif, wet, (1,))
+    forecast(f0, f1, dif, wet, pt, ((7, 10), 3), ((8, 10), 2))
+    aim(grid, a_ref, hot, obs, wc)
+    for o in (1, 3, 2):
+        for dg in (0, 2):
+            arrival(dg, o)
+    for h in (0, 2):
+        for dg in (0, 2):
+            passed_on(h, dg, True)
+    assemble(grid, g_ref, a_ref, f0, dif, wet, (0, 2))
+    forecast(f0, f1, dif, wet, pt, ((1, 13), 6), ((2, 12), 6))
+    analyse(grid, y_ref, pt, hot, obs, slab, wc, *scratch[9:])
 
     for o in range(1, LEVELS):
         start(pltpu.make_async_remote_copy(
@@ -217,23 +241,45 @@
     return jnp.concatenate(parts + [jnp.zeros((8, value.shape[1]), F32)], axis=0)
 
 
-def compute_kernel(n_gx, n_gy, g_ref, a_ref, ob_ref, out_ref, f0, f1, dif, wet, pt, mean, slab, wc, gram, tr, tv, ps, zs):
+def masks(n_gx, n_gy):
     gx, gy = lax.axis_index("gx"), lax.axis_index("gy")
-    up = jnp.where(gx > 0, 1.0, 0.0).astype(F32)
-    down = jnp.where(gx < n_gx - 1, 1.0, 0.0).astype(F32)
-    west = jnp.where(gy > 0, 1.0, 0.0).astype(F32)
-    east = jnp.where(gy < n_gy - 1, 1.0, 0.0).astype(F32)
-    in_grid = (up, jnp.float32(1.0), down)
+    one = lambda c: jnp.where(c, 1.0, 0.0).astype(F32)
     lane1 = iota((1, 128), 1)
-    beside = jnp.where(lane1 < 64, east, west)
+    in_grid = (one(gx > 0), jnp.float32(1.0), one(gx < n_gx - 1))
+    return in_grid, jnp.where(lane1 < 64, one(gy < n_gy - 1), one(gy > 0)), lane1
+
+
+def weigh(ob_ref, wc):
+    third = lax.rem(iota((1, 384), 1) >> 4, 3)
+    for a in range(2):
+        for r in range(3):
+            near = []
+            for c in range(3):
+                code = 3 * r + c
+                taper = 1.0 if code == 4 else 0.5 if (r == 1 or c == 1) else 0.25
+                chosen = jnp.zeros((1, 256), F32)
+                for s in range(5):
+                    blocks = ob_ref[5 * a + s:5 * a + s + 1, :]
+                    chosen = chosen + jnp.where(blocks == code, taper, 0.0)
+                chosen = jnp.concatenate([chosen, jnp.zeros((1, 128), F32)], axis=1)
+                near.append(pltpu.roll(chosen, (16 * (c - 1)) % 384, 1) if c != 1 else chosen)
+            for i in range(3):
+                which = lax.rem(third + 4 - i, 3)
+                wc[a, 3 * r + i:3 * r + i + 1, :] = jnp.where(
+                    which == 0, near[0], jnp.where(which == 1, near[1], near[2]))
+
+
+def assemble(grid, g_ref, a_ref, f0, dif, wet, groups):
+    in_grid, beside, lane1 = grid
 
     def both(h_of, dg):
-        own = h_of(1) * in_grid[dg]
-        side = jnp.where(lane1 < 64, h_of(2), h_of(0)) * (beside * in_grid[dg])
-        return own, side
+        own, side = h_of(1), jnp.where(lane1 < 64, h_of(2), h_of(0)) * (beside * in_grid[dg])
+        return (own if dg == 1 else own * in_grid[dg]), side
 
     for t in range(20):
         dg, r = (0, t + 2) if t < 6 else (1, t - 6) if t < 14 else (2, t - 14)
+        if dg not in groups:
+            continue
         main = 8 * r if r < 2 else 16 + 8 * r
         rest = 16 + 2 * r
         for s in range(LEVELS):
@@ -250,35 +296,36 @@
         wet[t, :, 0:128] = own
         wet[t, :, 128:256] = side
 
-    def advance(src, t):
-        c = src[t]
-        around = src[t + 1] + src[t - 1]
-        around = around + pltpu.roll(c, 255, 1) + pltpu.roll(c, 1, 1)
-        return wet[t] * (c + dif[t] * (around - 4.0 * c))
-
-    def first(t, carry):
-        f1[t] = advance(f0, t)
+
+def advance(src, dif, wet, t):
+    c = src[t]
+    around = src[t + 1] + src[t - 1]
+    around = around + pltpu.roll(c, 255, 1) + pltpu.roll(c, 1, 1)
+    return wet[t] * (c + dif[t] * (around - 4.0 * c))
+
+
+def forecast(f0, f1, dif, wet, pt, first, second):
+    def one(k, carry):
+        for low in first[0]:
+            f1[low + k] = advance(f0, dif, wet, low + k)
         return carry
 
-    lax.fori_loop(1, 19, first, 0)
-
-    def second(p, carry):
-        for r in range(4):
-            value = advance(f1, 2 + 4 * p + r)
+    lax.fori_loop(0, first[1], one, 0)
+
+    def two(k, carry):
+        for low in second[0]:
+            value = advance(f1, dif, wet, low + k)
             m = jnp.sum(value, axis=0, keepdims=True) / MEMBERS
-            q = value - m
-            tail = jnp.where(iota((8, 256), 0) == 0, m, 0.0)
-            for k in range(2):
-                at = 512 * k + 128 * r
-                pt[p, 0:40, at:at + 128] = q[:, 128 * k:128 * k + 128]
-                pt[p, 40:48, at:at + 128] = tail[:, 128 * k:128 * k + 128]
-            mean[p, :, 128 * r:128 * r + 128] = m[:, 0:128]
+            pt[low + k - 2, 0:40, :] = value - m
+            pt[low + k - 2, 40:48, :] = jnp.where(iota((8, 256), 0) == 0, m, 0.0)
         return carry
 
-    lax.fori_loop(0, 4, second, 0)
-
+    lax.fori_loop(0, second[1], two, 0)
+
+
+def aim(grid, a_ref, hot, obs, wc):
+    in_grid, beside, lane1 = grid
     lane2 = iota((1, 256), 1)
-    inverse_of = []
     for p in range(4):
         dg, a = ((0, 1), (1, 0), (1, 1), (2, 0))[p]
 
@@ -288,138 +335,174 @@
             return own, jnp.where(lane1 < 64, a_ref[2, dg, at:at + 1, :], a_ref[0, dg, at + 1:at + 2, :])
 
         value, variance, cell = rows_of(0), rows_of(1), rows_of(2)
-        found = []
         for k, (lane, shift) in enumerate(((lane2, 0), (lane1, jnp.where(lane1 < 64, 0, 64)))):
             c = cell[k].astype(jnp.int32)
             target = (c >> 3) * 128 + ((lane >> 4) << 3) + (c & 7) + shift
-            hot = jnp.where(iota((512, lane.shape[1]), 0) == target, 1.0, 0.0).astype(F32)
-            high, low = split(pt[p, :, 512 * k:512 * k + 512])
-            both_parts = mxu(jnp.concatenate([high, low], axis=0), hot)
+            at, width = 256 * k, lane.shape[1]
+
+            def fill(n, carry):
+                top = pl.multiple_of(n * 64, 64)
+                hot[p, pl.ds(top, 64), at:at + width] = jnp.where(
+                    iota((64, width), 0) == target - n * 64, 1.0, 0.0).astype(F32)
+                return carry
+
+            lax.fori_loop(0, 8, fill, 0)
+        obs[p:p + 1, :] = jnp.concatenate(value, axis=1)
+        inside = jnp.concatenate([jnp.ones((1, 256), F32), beside], axis=1) * in_grid[dg]
+        obs[4 + p:5 + p, :] = inside / jnp.concatenate(variance, axis=1)
+    for a in range(2):
+        for r in range(3):
+            p = a + r
+            rows = wc[a, 3 * r:3 * r + 3, :] * obs[4 + p:5 + p, :]
+            wc[a, 3 * r:3 * r + 3, :] = pltpu.roll(rows, 80 * (p % 3), 1) if p % 3 else rows
+
+
+GROUPS = 11
+
+
+def analyse(grid, y_ref, pt, hot, obs, slab, wc, gram, tr, tv, ps, zs):
+    lane1 = grid[2]
+
+    for p in range(4):
+        found = []
+        for k, (low, high) in enumerate(((0, 256), (256, 384))):
+            rows = jnp.concatenate([pt[4 * p + r, :, 128 * k:128 * k + 128] for r in range(4)], axis=1)
+            both_parts = mxu(jnp.concatenate(split(rows), axis=0), hot[p, :, low:high])
             found.append(both_parts[0:48] + both_parts[48:96])
         whole = jnp.concatenate(found, axis=1)
-        values = jnp.concatenate(value, axis=1)
-        tail = whole[40:48]
-        tail = jnp.where(iota((8, 384), 0) == 0, values - tail, 0.0)
-        slab[p, 0:40, :] = whole[0:40]
-        slab[p, 40:48, :] = tail
-        inside = jnp.concatenate([jnp.ones((1, 256), F32), beside], axis=1) * in_grid[dg]
-        inverse_of.append(inside / jnp.concatenate(variance, axis=1))
-
-    third = lax.rem(iota((1, 384), 1) >> 4, 3)
-    for a in range(2):
-        for r in range(3):
-            near = []
-            for c in range(3):
-                code = 3 * r + c
-                taper = 1.0 if code == 4 else 0.5 if (r == 1 or c == 1) else 0.25
-                chosen = jnp.zeros((1, 256), F32)
-                for s in range(5):
-                    blocks = ob_ref[5 * a + s:5 * a + s + 1, :]
-                    chosen = chosen + jnp.where(blocks == code, taper, 0.0)
-                chosen = jnp.concatenate([chosen, jnp.zeros((1, 128), F32)], axis=1)
-                near.append(pltpu.roll(chosen, (16 * (c - 1)) % 384, 1) if c != 1 else chosen)
-            for i in range(3):
-                which = lax.rem(third + 4 - i, 3)
-                w = jnp.where(which == 0, near[0], jnp.where(which == 1, near[1], near[2]))
-                wc[a, 3 * r + i:3 * r + i + 1, :] = w * inverse_of[a + r]
-
-    slot = lane1 >> 4
+        tail = jnp.where(iota((8, 384), 0) == 0, obs[p:p + 1, :] - whole[40:48], 0.0)
+        whole = jnp.concatenate([whole[0:40], tail], axis=0)
+        slab[p] = pltpu.roll(whole, 80 * (p % 3), 1) if p % 3 else whole
+
+    lane2 = iota((1, 256), 1)
+    part = jnp.where(lane2 < 80, 0, jnp.where(lane2 < 160, 1, jnp.where(lane2 < 240, 2, 3)))
+    slot = (lane2 - 80 * part) >> 4
     block = block_of(lane1)
-    own_slot = [(slot >= i) & (slot <= i + 2) for i in range(3)]
     diagonal = (lane1 - 40 * block == iota((40, 128), 0)) & (lane1 < 120)
+
+    def keep(n, o):
+        system = jnp.where(diagonal, 1.0, 0.0) + o[0:40] / (MEMBERS - 1.0)
+        gram[n, 0:40, :] = system
+        gram[n, 40:48, :] = o[40:48] / (MEMBERS - 1.0)
+        tr[n:n + 1, :] = jnp.sum(jnp.where(diagonal, system, 0.0), axis=0, keepdims=True)
+
+    last = []
     for g in range(6):
         turn = (16 - 48 * g) % 384
 
         def window(x):
-            return (pltpu.roll(x, turn, 1) if turn else x)[:, 0:128]
+            return pltpu.roll(x, turn, 1)[:, 0:256]
 
         parts = [window(slab[p]) for p in range(4)]
         for a in range(2):
+            left = jnp.where(part == 0, parts[3 * a], jnp.where(part == 1, parts[1], parts[2]))
             weights = window(wc[a])
-            left = jnp.concatenate(parts[a:a + 3], axis=1)
             right = []
             for i in range(3):
-                right.append(jnp.concatenate([
-                    parts[a + r][0:40] * jnp.where(own_slot[i], weights[3 * r + i:3 * r + i + 1], 0.0)
-                    for r in range(3)], axis=1))
-            right.append(jnp.zeros((8, 384), F32))
+                w = jnp.zeros((1, 256), F32)
+                for r in range(3):
+                    w = jnp.where(part == (a + r) % 3, weights[3 * r + i:3 * r + i + 1], w)
+                w = jnp.where((part < 3) & (slot >= i) & (slot <= i + 2), w, 0.0)
+                right.append(left[0:40] * w)
+            right.append(jnp.zeros((8, 256), F32))
             right = jnp.concatenate(right, axis=0)
-            lh, ll = split(left)
-            rh, rl = split(right)
-            o = mxu_nt(jnp.concatenate([lh, ll], axis=0), jnp.concatenate([rh, rl], axis=0))
+            o = mxu_nt(jnp.concatenate(split(left), axis=0), jnp.concatenate(split(right), axis=0))
             o = o[0:48] + o[48:96]
             o = o[:, 0:128] + o[:, 128:256]
-            system = jnp.where(diagonal, 1.0, 0.0) + o[0:40] / (MEMBERS - 1.0)
-            n = a * 6 + g
-            gram[n, 0:40, :] = system
-            gram[n, 40:48, :] = o[40:48] / (MEMBERS - 1.0)
-            tr[n:n + 1, :] = jnp.sum(jnp.where(diagonal, system, 0.0), axis=0, keepdims=True)
+            if g < 5:
+                keep(2 * g + a, o)
+            else:
+                last.append(o)
+    keep(10, jnp.where(block == 0, last[0], jnp.where(block == 1, pltpu.roll(last[1], 40, 1), 0.0)))
+    tr[11:12, :] = jnp.ones((1, 128), F32)
 
     rows = tr[...]
     sums = [jnp.sum(jnp.where(block == i, rows, 0.0), axis=1, keepdims=True) for i in range(3)]
     tv[...] = jnp.where(block == 0, sums[0], jnp.where(block == 1, sums[1], sums[2]))
-    for n in range(12):
+    for n in range(GROUPS):
         ps[n] = gram[n, 0:40, :] / tv[n:n + 1, :]
         zs[n] = jnp.where(diagonal, 1.0, 0.0)
 
     wide = jnp.concatenate([block, block], axis=1)
 
+    def times(rows_of, stacked, by_rows):
+        count = len(rows_of)
+        if by_rows:
+            o = mxu(jnp.concatenate([x for v in rows_of for x in split(v)], axis=0), stacked)
+            o = [o[80 * k:80 * k + 40] + o[80 * k + 40:80 * k + 80] for k in range(count)]
+        else:
+            o = mxu(jnp.concatenate([jnp.concatenate(split(v), axis=1) for v in rows_of], axis=0),
+                    jnp.concatenate([stacked, stacked], axis=0))
+            o = [o[40 * k:40 * k + 40] for k in range(count)]
+        return [x[:, 0:128] + x[:, 128:256] for x in o]
+
     def sweep(step, carry):
-        for n in range(12):
+        for n in range(GROUPS):
             p, z = ps[n], zs[n]
-            pair = jnp.concatenate(split(p), axis=1)
-            stacked = three_high(pair, wide)
-            right = jnp.concatenate([stacked, stacked], axis=0)
-            o = mxu(jnp.concatenate([pair, jnp.concatenate(split(z), axis=1)], axis=0), right)
-            o = o[:, 0:128] + o[:, 128:256]
-            zs[n] = 1.5 * z - 0.5 * o[40:80]
-            q = 1.5 * p - 0.5 * o[0:40]
-            o = mxu(jnp.concatenate(split(q), axis=1), right)
-            ps[n] = 1.5 * q - 0.5 * (o[:, 0:128] + o[:, 128:256])
+            stacked = three_high(jnp.concatenate(split(p), axis=1), wide)
+            pp, zp = times([p, z], stacked, BY_ROWS[0])
+            zs[n] = 1.5 * z - 0.5 * zp
+            q = 1.5 * p - 0.5 * pp
+            ps[n] = 1.5 * q - 0.5 * times([q], stacked, BY_ROWS[1])[0]
         return carry
 
     lax.fori_loop(0, NS_ITERS - 1, sweep, 0)
 
     ones = jnp.where((block_of(iota((128, 128), 0)) == block) & (lane1 < 120), 1.0, 0.0).astype(F32)
-    ones = jnp.concatenate([ones, ones], axis=0)
+    spreads, columns = [], []
+    for n in range(GROUPS):
+        z = zs[n]
+        stacked = three_high(jnp.concatenate(split(ps[n]), axis=1), wide)
+        z = 1.5 * z - 0.5 * times([z], stacked, BY_ROWS[2])[0]
+        spreads.append(z / jnp.sqrt(tv[n:n + 1, :]))
+        columns.append(jnp.concatenate(split(spreads[n] * gram[n, 40:41, :]), axis=1))
+    partial = mxu(jnp.concatenate(columns, axis=0), jnp.concatenate([ones, ones], axis=0))
+    transforms = []
+    for n in range(GROUPS):
+        centre = jnp.sum(spreads[n] * partial[40 * n:40 * n + 40], axis=0, keepdims=True)
+        th, tl = split(spreads[n] + centre)
+        transforms.append(jnp.concatenate([
+            jnp.concatenate([th, th], axis=1), jnp.concatenate([tl, jnp.zeros_like(tl)], axis=1)], axis=0))
+
     patch = lax.rem(iota((1, 512), 1), 128) >> 3
+    flat = y_ref.reshape(MEMBERS * 8, 128)
     for a in range(2):
-        total = jnp.zeros((40, 512), F32)
-        ph, plow = split(pt[a + 1, 0:40, 0:512])
+        here = jnp.concatenate([pt[4 + 4 * a + r, 0:40, 0:128] for r in range(4)], axis=1)
+        here = split(here)
+        total = jnp.zeros((80, 512), F32)
         for g in range(6):
-            n = a * 6 + g
-            p, z = ps[n], zs[n]
-            pair = jnp.concatenate(split(p), axis=1)
-            stacked = three_high(pair, wide)
-            o = mxu(jnp.concatenate(split(z), axis=1), jnp.concatenate([stacked, stacked], axis=0))
-            z = 1.5 * z - 0.5 * (o[:, 0:128] + o[:, 128:256])
-            spread = z / jnp.sqrt(tv[n:n + 1, :])
-            partial = mxu(jnp.concatenate(split(spread * gram[n, 40:41, :]), axis=1), ones)
-            centre = jnp.sum(spread * partial, axis=0, keepdims=True)
-            th, tl = split(spread + centre)
-            high = three_high_by(ph, patch, 3 * g)
-            low = three_high_by(plow, patch, 3 * g)
-            total = total + mxu(jnp.concatenate([th, tl, th], axis=1), jnp.concatenate([high, high, low], axis=0))
-        total = total + mean[a + 1]
-        flat = out_ref.reshape(MEMBERS * 8, 128)
+            n = 2 * g + a if g < 5 else 10
+            ids = (3 * g, 3 * g + 1, 3 * g + 2) if g < 5 else (15, -1, -1) if a == 0 else (-1, 15, -1)
+            pieces = []
+            for v in here:
+                pieces += [jnp.where(patch == c, v, 0.0) if c >= 0 else jnp.zeros((40, 512), F32) for c in ids]
+                pieces.append(jnp.zeros((8, 512), F32))
+            total = total + mxu(transforms[n], jnp.concatenate(pieces, axis=0))
+        total = total[0:40] + total[40:80]
         for r in range(4):
-            value = total[:, 128 * r:128 * r + 128]
+            value = total[:, 128 * r:128 * r + 128] + pt[4 + 4 * a + r, 40:41, 0:128]
             for s in range(LEVELS):
                 flat[pl.ds(80 * s + 4 * a + r, 8, stride=8), :] = value[8 * s:8 * s + 8]
                 flat[pl.ds(80 * s + 64 + 4 * a + r, 2, stride=8), :] = value[32 + 2 * s:34 + 2 * s]
 
 
-def three_high_by(value, patch, first):
-    parts = [jnp.where(patch == first + i, value, 0.0) for i in range(3)]
-    return jnp.concatenate(parts + [jnp.zeros((8, value.shape[1]), F32)], axis=0)
+def compute_kernel(n_gx, n_gy, g_ref, a_ref, ob, y_ref, f0, f1, dif, wet, pt, hot, obs, slab, wc, *rest):
+    grid = masks(n_gx, n_gy)
+    weigh(ob, wc)
+    aim(grid, a_ref, hot, obs, wc)
+    assemble(grid, g_ref, a_ref, f0, dif, wet, (1,))
+    forecast(f0, f1, dif, wet, pt, ((7, 10), 3), ((8, 10), 2))
+    assemble(grid, g_ref, a_ref, f0, dif, wet, (0, 2))
+    forecast(f0, f1, dif, wet, pt, ((1, 13), 6), ((2, 12), 6))
+    analyse(grid, y_ref, pt, hot, obs, slab, wc, *rest)
 
 
 def scratch_of():
     return [
         pltpu.VMEM((20, 40, 256), F32), pltpu.VMEM((20, 40, 256), F32),
         pltpu.VMEM((20, 1, 256), F32), pltpu.VMEM((20, 1, 256), F32),
-        pltpu.VMEM((4, 48, 1024), F32), pltpu.VMEM((4, 1, 512), F32),
-        pltpu.VMEM((4, 48, 384), F32), pltpu.VMEM((2, 9, 384), F32),
+        pltpu.VMEM((16, 48, 256), F32), pltpu.VMEM((4, 512, 384), F32), pltpu.VMEM((8, 384), F32),
+        pltpu.VMEM((4, 48, 384), F32), pltpu.VMEM((2, 16, 384), F32),
         pltpu.VMEM((12, 48, 128), F32), pltpu.VMEM((12, 128), F32), pltpu.VMEM((12, 128), F32),
         pltpu.VMEM((12, 40, 128), F32), pltpu.VMEM((12, 40, 128), F32)]
 

time: 55.6 us -> 52 us (0.935)
  the two profiles are of different devices: /device:TPU:9 before, /device:TPU:26 now
where the time goes in v3:
time: 52 us; the launch traced here: 51.8 us
  Pallas kernels  50.2 us (97%)
  local copies, waits for them, and re-layouts  1.59 us (3%)
    pallas_call x1, Pallas kernels, local(): pl.pallas_call(body, out_shape=jax.ShapeDtypeStruct((OWN, LEVELS, 8, 128)...  50.2 us
    unnamed x1, local copies, waits for them, and re-layouts  1.59 us

profile of v3, /device:TPU:26, one launch (start us, length us, event | category | flops | bytes accessed | tf_op | source)
XLA Modules:
  0.0 51.8 jit_solution(17896861650055326321)
XLA Ops:
  0.0 50.2 %cycle.1 = f32[10,4,8,128]{3,2,1,0:T(8,128)} custom-call(f32[10,4,8,128]{3,2,1,0:T(8,128)} %refs_0_.1, f32[4,8,128]{2,1,0:T(8,128)} %refs_1_.1, s32[8,128]{1,0:T(8,128)} %refs_2_.1, f32[4,16,2,16]{3,2,1,0:T(2,128)} %refs_3_.1, f32[4,16,2,16]{3,2,1,0:T(2,128)} %refs_4_.1, s32[4,16,2,16]{3,2,1,0:T(2,128)} %refs_5_.1, s32[5,2,16]{2,1,0:T(2,128)} %refs_6_.1), custom_call_target="tpu_custom_call" | custom-call | tf_op jit(solution)/shard_map/cycle/pallas_call | solution.py:518
  50.2 1.6 %copy.9 = f32[10,4,8,128]{3,2,1,0:T(8,128)} copy(f32[10,4,8,128]{3,2,1,0:T(8,128)} %cycle.1) | data formatting | bytes 327680

commit v4 on v3

--- a/solution.py
+++ b/solution.py
@@ -13,8 +13,14 @@
 OWN = 10
 MEMBERS = 40
 OBS = 16
-AUX = 32
-NEED = ((16, 64), (0, 80), (0, 64))
+MAIN = (64, 72, 20, 28, 36, 44, 0, 8)
+REST = (60, 62, 52, 54, 56, 58, 16, 18)
+AUX = 28
+FLOW = (6, 7, 10, 11, 12, 13, 18, 19)
+WET = (8, 9, 14, 15, 16, 17, 20, 21)
+SEEN = (0, 22)
+NEED = ((0, 60), (0, 80), (20, 60))
+NEED_AUX = ((10, 18), (0, 28), (0, 18))
 
 
 def neighbours(n_gx, n_gy):
@@ -26,15 +32,18 @@
     return mem, gx, gy, rows, sides, there, back
 
 
-def prepare(level, x_ref, dif_ref, mask_ref, val_ref, var_ref, cell_ref, blk_ref, xs, aux, ob):
+def lay_out(x_ref, xs):
     flat = x_ref.reshape(OWN * LEVELS * 8, 128)
     for k in range(LEVELS):
         for r in range(8):
-            main = 8 * r if r < 2 else 16 + 8 * r
-            xs[k, main:main + 8, :] = flat[pl.ds(k * 8 + r, 8, stride=32), :]
-            xs[k, 16 + 2 * r:18 + 2 * r, :] = flat[pl.ds(256 + k * 8 + r, 2, stride=32), :]
-    aux[0:8, :] = dif_ref[level]
-    aux[8:16, :] = mask_ref[...].astype(F32)
+            xs[k, MAIN[r]:MAIN[r] + 8, :] = flat[pl.ds(k * 8 + r, 8, stride=32), :]
+            xs[k, REST[r]:REST[r] + 2, :] = flat[pl.ds(256 + k * 8 + r, 2, stride=32), :]
+
+
+def prepare(level, dif_ref, mask_ref, val_ref, var_ref, cell_ref, blk_ref, aux, ob):
+    for rows, value in ((FLOW, dif_ref[level]), (WET, mask_ref[...].astype(F32))):
+        for r in range(8):
+            aux[rows[r]:rows[r] + 1, :] = value[r:r + 1]
     spread_out = jnp.where(iota((16, 256), 0) == iota((16, 256), 1) >> 4, 1.0, 0.0).astype(F32)
     kinds = [ref[level].astype(F32) for ref in (val_ref, var_ref, cell_ref)]
     stacked = jnp.concatenate([kinds[k][:, a, :] for a in range(2) for k in range(3)], axis=0)
@@ -43,9 +52,9 @@
     mine = iota((16, 256), 0) == (iota((16, 256), 1) & 15)
     for n in range(6):
         row = jnp.sum(jnp.where(mine, wide[16 * n:16 * n + 16], 0.0), axis=0, keepdims=True)
-        aux[16 + 2 * n:17 + 2 * n, :] = row[:, 0:128]
-        aux[17 + 2 * n:18 + 2 * n, :] = row[:, 128:256]
-    aux[28:32, :] = jnp.zeros((4, 128), F32)
+        at = SEEN[n // 3] + 2 * (n % 3)
+        aux[at:at + 1, :] = row[:, 0:128]
+        aux[at + 1:at + 2, :] = row[:, 128:256]
     blocks = blk_ref[...].astype(F32)
     blocks = jnp.concatenate([blocks[:, a, :] for a in range(2)] + [jnp.zeros((6, 16), F32)], axis=0)
     ob[...] = mxu(blocks, spread_out)
@@ -85,22 +94,10 @@
         (cell_any, cell_ref), (blk_any, blk_ref)))]
     for load in loads:
         load.start()
-    for load in loads:
-        load.wait()
-    prepare(mem, x_ref, dif_ref, mask_ref, val_ref, var_ref, cell_ref, blk_ref, xs, aux, ob)
+    loads[0].wait()
+    lay_out(x_ref, xs)
     f0, f1, dif, wet, pt, hot, obs, slab, wc = scratch[:9]
     grid = masks(n_gx, n_gy)
-    for dg in (0, 2):
-        @when(~in_rows[dg])
-        def _():
-            for h in range(3):
-                g_ref[h, dg] = jnp.zeros((LEVELS, 80, 128), F32)
-                a_ref[h, dg] = jnp.ones((AUX, 128), F32)
-    for h in (0, 2):
-        @when(~in_sides[h // 2])
-        def _():
-            g_ref[h] = jnp.zeros((3, LEVELS, 80, 128), F32)
-            a_ref[h] = jnp.ones((3, AUX, 128), F32)
     pl.semaphore_wait(barrier, count)
 
     sends = []
@@ -112,7 +109,7 @@
     def forward(source, dg, slot, part, index):
         for e, side in enumerate(sides):
             h = 2 if e == 0 else 0
-            dst = a_ref.at[h, dg] if slot is None else g_ref.at[h, dg, slot, part]
+            dst = a_ref.at[h, dg, part] if slot is None else g_ref.at[h, dg, slot, part]
             start(pltpu.make_async_remote_copy(
                 src_ref=source, dst_ref=dst, send_sem=fsem.at[e, dg, index], recv_sem=frsem.at[h // 2, dg, index],
                 device_id=(mem, gx, side), device_id_type=MESH), in_rows[dg], in_sides[e])
@@ -131,17 +128,32 @@
                 device_id=(mem, rows[d], gy), device_id_type=MESH), in_rows[d])
 
     def scatter_aux(d):
+        part = pl.ds(*NEED_AUX[2 - d])
         start(pltpu.make_async_remote_copy(
-            src_ref=aux, dst_ref=a_ref.at[1, 2 - d], send_sem=asem.at[d], recv_sem=arsem.at[2 - d],
+            src_ref=aux.at[part], dst_ref=a_ref.at[1, 2 - d, part], send_sem=asem.at[d], recv_sem=arsem.at[2 - d],
             device_id=(mem, rows[d], gy), device_id_type=MESH), in_rows[d])
 
-    forward(aux, 1, None, None, LEVELS)
-    forward(xs.at[mem], 1, mem, pl.ds(0, 80), 0)
-    for o in range(1, LEVELS):
+    for o in (2, 1, 3):
         scatter(o)
     halo(xs.at[mem], mem, 0)
+    forward(xs.at[mem], 1, mem, pl.ds(0, 80), 0)
+    for load in loads[1:]:
+        load.wait()
+    prepare(mem, dif_ref, mask_ref, val_ref, var_ref, cell_ref, blk_ref, aux, ob)
     for d in (0, 2):
         scatter_aux(d)
+    forward(aux, 1, None, pl.ds(*NEED_AUX[1]), LEVELS)
+    for dg in (0, 2):
+        @when(~in_rows[dg])
+        def _():
+            for h in range(3):
+                g_ref[h, dg] = jnp.zeros((LEVELS, 80, 128), F32)
+                a_ref[h, dg] = jnp.ones((AUX, 128), F32)
+    for h in (0, 2):
+        @when(~in_sides[h // 2])
+        def _():
+            g_ref[h] = jnp.zeros((3, LEVELS, 80, 128), F32)
+            a_ref[h] = jnp.ones((3, AUX, 128), F32)
     g_ref[1, 1, mem] = xs[mem]
     a_ref[1, 1] = aux[...]
 
@@ -161,12 +173,14 @@
     for o in (1, 3, 2):
         arrival(1, o)
     for dg in (0, 2):
+        part = pl.ds(*NEED_AUX[dg])
+
         @when(in_rows[dg])
         def _():
             pltpu.make_async_remote_copy(
-                src_ref=aux, dst_ref=a_ref.at[1, dg], send_sem=asem.at[dg], recv_sem=arsem.at[dg],
+                src_ref=aux.at[part], dst_ref=a_ref.at[1, dg, part], send_sem=asem.at[dg], recv_sem=arsem.at[dg],
                 device_id=(mem, rows[dg], gy), device_id_type=MESH).wait_recv()
-        forward(a_ref.at[1, dg], dg, None, None, LEVELS)
+        forward(a_ref.at[1, dg, part], dg, None, part, LEVELS)
     def passed_on(h, dg, chunks):
         @when(in_sides[h // 2], in_rows[dg])
         def _():
@@ -178,7 +192,7 @@
                     device_id=(mem, gx, sides[0]), device_id_type=MESH).wait_recv()
             if not chunks:
                 pltpu.make_async_remote_copy(
-                    src_ref=aux, dst_ref=a_ref.at[h, dg],
+                    src_ref=aux.at[pl.ds(*NEED_AUX[dg])], dst_ref=a_ref.at[h, dg, pl.ds(*NEED_AUX[dg])],
                     send_sem=fsem.at[0, dg, LEVELS], recv_sem=frsem.at[h // 2, dg, LEVELS],
                     device_id=(mem, gx, sides[0]), device_id_type=MESH).wait_recv()
 
@@ -200,17 +214,23 @@
             passed_on(h, dg, True)
     assemble(grid, g_ref, a_ref, f0, dif, wet, (0, 2))
     forecast(f0, f1, dif, wet, pt, ((1, 13), 6), ((2, 12), 6))
-    analyse(grid, y_ref, pt, hot, obs, slab, wc, *scratch[9:])
-
-    for o in range(1, LEVELS):
-        start(pltpu.make_async_remote_copy(
-            src_ref=y_ref.at[there[o]], dst_ref=out_ref.at[:, mem], send_sem=bsem.at[o], recv_sem=brsem.at[o],
-            device_id=(there[o], gx, gy), device_id_type=MESH))
+    def give_back(a):
+        part = pl.ds(4 * a, 4)
+        for o in (2, 1, 3):
+            start(pltpu.make_async_remote_copy(
+                src_ref=y_ref.at[there[o], :, part], dst_ref=out_ref.at[:, mem, part],
+                send_sem=bsem.at[a, o], recv_sem=brsem.at[a, o],
+                device_id=(there[o], gx, gy), device_id_type=MESH))
+
+    analyse(grid, y_ref, give_back, pt, hot, obs, slab, wc, *scratch[9:])
     out_ref[:, mem] = y_ref[mem]
-    for o in range(1, LEVELS):
-        pltpu.make_async_remote_copy(
-            src_ref=y_ref.at[0], dst_ref=out_ref.at[:, back[o]], send_sem=bsem.at[o], recv_sem=brsem.at[o],
-            device_id=(there[o], gx, gy), device_id_type=MESH).wait_recv()
+    for a in range(2):
+        for o in range(1, LEVELS):
+            part = pl.ds(4 * a, 4)
+            pltpu.make_async_remote_copy(
+                src_ref=y_ref.at[0, :, part], dst_ref=out_ref.at[:, back[o], part],
+                send_sem=bsem.at[a, o], recv_sem=brsem.at[a, o],
+                device_id=(there[o], gx, gy), device_id_type=MESH).wait_recv()
     for copy, conditions in sends:
         when(*conditions)(copy.wait_send)
 
@@ -280,8 +300,7 @@
         dg, r = (0, t + 2) if t < 6 else (1, t - 6) if t < 14 else (2, t - 14)
         if dg not in groups:
             continue
-        main = 8 * r if r < 2 else 16 + 8 * r
-        rest = 16 + 2 * r
+        main, rest = MAIN[r], REST[r]
         for s in range(LEVELS):
             own, side = both(lambda h: g_ref[h, dg, s, main:main + 8, :], dg)
             f0[t, 8 * s:8 * s + 8, 0:128] = own
@@ -289,10 +308,10 @@
             own, side = both(lambda h: g_ref[h, dg, s, rest:rest + 2, :], dg)
             f0[t, 32 + 2 * s:34 + 2 * s, 0:128] = own
             f0[t, 32 + 2 * s:34 + 2 * s, 128:256] = side
-        own, side = both(lambda h: a_ref[h, dg, r:r + 1, :], dg)
+        own, side = both(lambda h: a_ref[h, dg, FLOW[r]:FLOW[r] + 1, :], dg)
         dif[t, :, 0:128] = own
         dif[t, :, 128:256] = side
-        own, side = both(lambda h: a_ref[h, dg, 8 + r:9 + r, :], dg)
+        own, side = both(lambda h: a_ref[h, dg, WET[r]:WET[r] + 1, :], dg)
         wet[t, :, 0:128] = own
         wet[t, :, 128:256] = side
 
@@ -330,7 +349,7 @@
         dg, a = ((0, 1), (1, 0), (1, 1), (2, 0))[p]
 
         def rows_of(kind):
-            at = 16 + (a * 3 + kind) * 2
+            at = SEEN[a] + 2 * kind
             own = jnp.concatenate([a_ref[1, dg, at:at + 1, :], a_ref[1, dg, at + 1:at + 2, :]], axis=1)
             return own, jnp.where(lane1 < 64, a_ref[2, dg, at:at + 1, :], a_ref[0, dg, at + 1:at + 2, :])
 
@@ -360,7 +379,7 @@
 GROUPS = 11
 
 
-def analyse(grid, y_ref, pt, hot, obs, slab, wc, gram, tr, tv, ps, zs):
+def analyse(grid, y_ref, done, pt, hot, obs, slab, wc, gram, tr, tv, ps, zs):
     lane1 = grid[2]
 
     for p in range(4):
@@ -484,6 +503,7 @@
             for s in range(LEVELS):
                 flat[pl.ds(80 * s + 4 * a + r, 8, stride=8), :] = value[8 * s:8 * s + 8]
                 flat[pl.ds(80 * s + 64 + 4 * a + r, 2, stride=8), :] = value[32 + 2 * s:34 + 2 * s]
+        done(a)
 
 
 def compute_kernel(n_gx, n_gy, g_ref, a_ref, ob, y_ref, f0, f1, dif, wet, pt, hot, obs, slab, wc, *rest):
@@ -494,7 +514,7 @@
     forecast(f0, f1, dif, wet, pt, ((7, 10), 3), ((8, 10), 2))
     assemble(grid, g_ref, a_ref, f0, dif, wet, (0, 2))
     forecast(f0, f1, dif, wet, pt, ((1, 13), 6), ((2, 12), 6))
-    analyse(grid, y_ref, pt, hot, obs, slab, wc, *rest)
+    analyse(grid, y_ref, lambda a: None, pt, hot, obs, slab, wc, *rest)
 
 
 def scratch_of():
@@ -523,7 +543,7 @@
                 pltpu.VMEM((3, 3, LEVELS, 80, 128), F32), pltpu.VMEM((3, 3, AUX, 128), F32),
                 pltpu.VMEM((LEVELS, OWN, 8, 128), F32)] + scratch_of() + [
                 dma((3, LEVELS)), dma((3, LEVELS)), dma((3,)), dma((3,)),
-                dma((2, 3, LEVELS + 1)), dma((2, 3, LEVELS + 1)), dma((7,)), dma((LEVELS,)), dma((LEVELS,))],
+                dma((2, 3, LEVELS + 1)), dma((2, 3, LEVELS + 1)), dma((7,)), dma((2, LEVELS)), dma((2, LEVELS))],
             compiler_params=pltpu.CompilerParams(collective_id=0, has_side_effects=True),
             name="cycle")(*args)
 

time: 52 us -> 50.5 us (0.971)
  the two profiles are of different devices: /device:TPU:26 before, /device:TPU:19 now
where the time goes in v4:
time: 50.5 us; the launch traced here: 49.9 us
  Pallas kernels  48.3 us (96%)
  local copies, waits for them, and re-layouts  1.59 us (3%)
    pallas_call x1, Pallas kernels, local(): pl.pallas_call(body, out_shape=jax.ShapeDtypeStruct((OWN, LEVELS, 8, 128)...  48.3 us
    unnamed x1, local copies, waits for them, and re-layouts  1.59 us

profile of v4, /device:TPU:19, one launch (start us, length us, event | category | flops | bytes accessed | tf_op | source)
XLA Modules:
  0.0 49.9 jit_solution(10217262091728662445)
XLA Ops:
  0.0 48.3 %cycle.1 = f32[10,4,8,128]{3,2,1,0:T(8,128)} custom-call(f32[10,4,8,128]{3,2,1,0:T(8,128)} %refs_0_.1, f32[4,8,128]{2,1,0:T(8,128)} %refs_1_.1, s32[8,128]{1,0:T(8,128)} %refs_2_.1, f32[4,16,2,16]{3,2,1,0:T(2,128)} %refs_3_.1, f32[4,16,2,16]{3,2,1,0:T(2,128)} %refs_4_.1, s32[4,16,2,16]{3,2,1,0:T(2,128)} %refs_5_.1, s32[5,2,16]{2,1,0:T(2,128)} %refs_6_.1), custom_call_target="tpu_custom_call" | custom-call | tf_op jit(solution)/shard_map/cycle/pallas_call | solution.py:538
  48.3 1.6 %copy.9 = f32[10,4,8,128]{3,2,1,0:T(8,128)} copy(f32[10,4,8,128]{3,2,1,0:T(8,128)} %cycle.1) | data formatting | bytes 327680

commit v5 on v4

--- a/solution.py
+++ b/solution.py
@@ -9,6 +9,8 @@
 F32 = jnp.float32
 NS_ITERS = 7
 BY_ROWS = (False, False, False)
+SWEEP_UNROLL = 6
+FORECAST_UNROLL = 2
 LEVELS = 4
 OWN = 10
 MEMBERS = 40
@@ -329,7 +331,7 @@
             f1[low + k] = advance(f0, dif, wet, low + k)
         return carry
 
-    lax.fori_loop(0, first[1], one, 0)
+    lax.fori_loop(0, first[1], one, 0, unroll=FORECAST_UNROLL)
 
     def two(k, carry):
         for low in second[0]:
@@ -339,7 +341,7 @@
             pt[low + k - 2, 40:48, :] = jnp.where(iota((8, 256), 0) == 0, m, 0.0)
         return carry
 
-    lax.fori_loop(0, second[1], two, 0)
+    lax.fori_loop(0, second[1], two, 0, unroll=FORECAST_UNROLL)
 
 
 def aim(grid, a_ref, hot, obs, wc):
@@ -465,7 +467,7 @@
             ps[n] = 1.5 * q - 0.5 * times([q], stacked, BY_ROWS[1])[0]
         return carry
 
-    lax.fori_loop(0, NS_ITERS - 1, sweep, 0)
+    lax.fori_loop(0, NS_ITERS - 1, sweep, 0, unroll=SWEEP_UNROLL)
 
     ones = jnp.where((block_of(iota((128, 128), 0)) == block) & (lane1 < 120), 1.0, 0.0).astype(F32)
     spreads, columns = [], []

time: 50.5 us -> 48.5 us (0.960)
  Pallas kernels: 48.3 us -> 46.7 us
    pallas_call x1, Pallas kernels: 48.3 us -> 46.7 us  [local(): pl.pallas_call(body, out_shape=jax.ShapeDtypeStruct((OWN, LEVELS, 8, 128)...]
where the time goes in v5:
time: 48.5 us; the launch traced here: 48.3 us
  Pallas kernels  46.7 us (96%)
  local copies, waits for them, and re-layouts  1.59 us (3%)
    pallas_call x1, Pallas kernels, local(): pl.pallas_call(body, out_shape=jax.ShapeDtypeStruct((OWN, LEVELS, 8, 128)...  46.7 us
    unnamed x1, local copies, waits for them, and re-layouts  1.59 us

profile of v5, /device:TPU:19, one launch (start us, length us, event | category | flops | bytes accessed | tf_op | source)
XLA Modules:
  0.0 48.3 jit_solution(14582939728006024263)
XLA Ops:
  0.0 46.7 %cycle.1 = f32[10,4,8,128]{3,2,1,0:T(8,128)} custom-call(f32[10,4,8,128]{3,2,1,0:T(8,128)} %refs_0_.1, f32[4,8,128]{2,1,0:T(8,128)} %refs_1_.1, s32[8,128]{1,0:T(8,128)} %refs_2_.1, f32[4,16,2,16]{3,2,1,0:T(2,128)} %refs_3_.1, f32[4,16,2,16]{3,2,1,0:T(2,128)} %refs_4_.1, s32[4,16,2,16]{3,2,1,0:T(2,128)} %refs_5_.1, s32[5,2,16]{2,1,0:T(2,128)} %refs_6_.1), custom_call_target="tpu_custom_call" | custom-call | tf_op jit(solution)/shard_map/cycle/pallas_call | solution.py:540
  46.7 1.6 %copy.9 = f32[10,4,8,128]{3,2,1,0:T(8,128)} copy(f32[10,4,8,128]{3,2,1,0:T(8,128)} %cycle.1) | data formatting | bytes 327680

commit v6 on v5

--- a/solution.py
+++ b/solution.py
@@ -9,7 +9,7 @@
 F32 = jnp.float32
 NS_ITERS = 7
 BY_ROWS = (False, False, False)
-SWEEP_UNROLL = 6
+SWEEP_UNROLL = 5
 FORECAST_UNROLL = 2
 LEVELS = 4
 OWN = 10
@@ -442,7 +442,6 @@
     tv[...] = jnp.where(block == 0, sums[0], jnp.where(block == 1, sums[1], sums[2]))
     for n in range(GROUPS):
         ps[n] = gram[n, 0:40, :] / tv[n:n + 1, :]
-        zs[n] = jnp.where(diagonal, 1.0, 0.0)
 
     wide = jnp.concatenate([block, block], axis=1)
 
@@ -457,6 +456,13 @@
             o = [o[40 * k:40 * k + 40] for k in range(count)]
         return [x[:, 0:128] + x[:, 128:256] for x in o]
 
+    for n in range(GROUPS):
+        p = ps[n]
+        stacked = three_high(jnp.concatenate(split(p), axis=1), wide)
+        zs[n] = jnp.where(diagonal, 1.5, 0.0) - 0.5 * p
+        q = 1.5 * p - 0.5 * times([p], stacked, BY_ROWS[0])[0]
+        ps[n] = 1.5 * q - 0.5 * times([q], stacked, BY_ROWS[1])[0]
+
     def sweep(step, carry):
         for n in range(GROUPS):
             p, z = ps[n], zs[n]
@@ -467,7 +473,7 @@
             ps[n] = 1.5 * q - 0.5 * times([q], stacked, BY_ROWS[1])[0]
         return carry
 
-    lax.fori_loop(0, NS_ITERS - 1, sweep, 0, unroll=SWEEP_UNROLL)
+    lax.fori_loop(0, NS_ITERS - 2, sweep, 0, unroll=SWEEP_UNROLL)
 
     ones = jnp.where((block_of(iota((128, 128), 0)) == block) & (lane1 < 120), 1.0, 0.0).astype(F32)
     spreads, columns = [], []

time: 48.5 us -> 48.5 us (level)
  no operation moved by 1% of the time
where the time goes in v6:
time: 48.5 us; the launch traced here: 48.3 us
  Pallas kernels  46.7 us (96%)
  local copies, waits for them, and re-layouts  1.59 us (3%)
    pallas_call x1, Pallas kernels, local(): pl.pallas_call(body, out_shape=jax.ShapeDtypeStruct((OWN, LEVELS, 8, 128)...  46.7 us
    unnamed x1, local copies, waits for them, and re-layouts  1.59 us

profile of v6, /device:TPU:19, one launch (start us, length us, event | category | flops | bytes accessed | tf_op | source)
XLA Modules:
  0.0 48.3 jit_solution(7399578756144866456)
XLA Ops:
  0.0 46.7 %cycle.1 = f32[10,4,8,128]{3,2,1,0:T(8,128)} custom-call(f32[10,4,8,128]{3,2,1,0:T(8,128)} %refs_0_.1, f32[4,8,128]{2,1,0:T(8,128)} %refs_1_.1, s32[8,128]{1,0:T(8,128)} %refs_2_.1, f32[4,16,2,16]{3,2,1,0:T(2,128)} %refs_3_.1, f32[4,16,2,16]{3,2,1,0:T(2,128)} %refs_4_.1, s32[4,16,2,16]{3,2,1,0:T(2,128)} %refs_5_.1, s32[5,2,16]{2,1,0:T(2,128)} %refs_6_.1), custom_call_target="tpu_custom_call" | custom-call | tf_op jit(solution)/shard_map/cycle/pallas_call | solution.py:546
  46.7 1.6 %copy.9 = f32[10,4,8,128]{3,2,1,0:T(8,128)} copy(f32[10,4,8,128]{3,2,1,0:T(8,128)} %cycle.1) | data formatting | bytes 327680
